TPU v7x, 32 devices: a 4x4x1 block of a 4x4x8 slice. The times are simulated.
32 devices in a mesh: dp: 1 (over z), tp: 4 (over y), ep: 8 (over x, core).
Axes of the slice: x: 4, y: 4, z: 1, core: 2. Of those that a mesh axis runs over, the one named last changes fastest.
The devices are a block of a 4x4x8 slice.
Arguments:
- x: bfloat16 [64, 1024, 768], P(('dp', 'ep'))
- src_len: int32 [64], P(('dp', 'ep'))
- expert_idx: int32 [64, 1024, 2], P(('dp', 'ep'))
- ln_gain: float32 [4, 768], replicated
- ln_bias: float32 [4, 768], replicated
- w_query: bfloat16 [2, 768, 12, 64], P(None, None, 'tp')
- b_query: float32 [2, 12, 64], P(None, 'tp')
- w_key: bfloat16 [2, 768, 12, 64], P(None, None, 'tp')
- w_value: bfloat16 [2, 768, 12, 64], P(None, None, 'tp')
- b_value: float32 [2, 12, 64], P(None, 'tp')
- w_attn_out: bfloat16 [2, 12, 64, 768], P(None, 'tp')
- b_attn_out: float32 [2, 768], replicated
- w_fc1: bfloat16 [768, 3072], P(None, 'tp')
- b_fc1: float32 [3072], P('tp')
- w_fc2: bfloat16 [3072, 768], P('tp')
- b_fc2: float32 [768], replicated
- w_router: float32 [768, 32], replicated
- w_exp_in: bfloat16 [32, 768, 3072], P('ep', None, 'tp')
- b_exp_in: float32 [32, 3072], P('ep', 'tp')
- w_exp_out: bfloat16 [32, 3072, 768], P('ep', 'tp')
- b_exp_out: float32 [32, 768], P('ep')
Outputs:
- output: bfloat16 [64, 1024, 768], P(('dp', 'ep'))
All inputs are finite; a program needn't handle non-finite values.
Results may differ from a plain program's by a relative error of at most 0.0144854.
Values are sent between devices in bfloat16 or wider.
A program may use at most 768 MiB of HBM per device.

v0:
```python
import jax
import jax.numpy as jnp
from jax import lax
from jax.sharding import PartitionSpec as P

LN_EPS = 1e-5


def layer_norm(hidden, gain, shift):
    hidden = hidden.astype(jnp.float32)
    centered = hidden - jnp.mean(hidden, axis=-1, keepdims=True)
    variance = jnp.mean(centered * centered, axis=-1, keepdims=True)
    return centered * lax.rsqrt(variance + LN_EPS) * gain + shift


def attention_layer(residual, key_ok, gain, shift, w_q, b_q, w_k, w_v, b_v, w_o, b_o):
    normed = layer_norm(residual, gain, shift).astype(jnp.bfloat16)
    query = (jnp.einsum('rsd,dhk->rshk', normed, w_q, preferred_element_type=jnp.float32) + b_q).astype(jnp.bfloat16)
    keys = jnp.einsum('rsd,dhk->rshk', normed, w_k, preferred_element_type=jnp.float32).astype(jnp.bfloat16)
    values = (jnp.einsum('rsd,dhk->rshk', normed, w_v, preferred_element_type=jnp.float32) + b_v).astype(jnp.bfloat16)
    scores = jnp.einsum('rqhk,rshk->rhqs', query, keys, preferred_element_type=jnp.float32) * (w_q.shape[-1] ** -0.5)
    scores = jnp.where(key_ok[:, None, None, :], scores, -1e30)
    attn_probs = jax.nn.softmax(scores, axis=-1).astype(jnp.bfloat16)
    context = jnp.einsum('rhqs,rshk->rqhk', attn_probs, values, preferred_element_type=jnp.float32).astype(jnp.bfloat16)
    partial = jnp.einsum('rqhk,hkd->rqd', context, w_o, preferred_element_type=jnp.float32).astype(jnp.bfloat16)
    total = lax.psum(partial, 'tp')
    return (residual.astype(jnp.float32) + total.astype(jnp.float32) + b_o).astype(jnp.bfloat16)


def dense_ffn(residual, gain, shift, w_in, b_in, w_out, b_out):
    normed = layer_norm(residual, gain, shift).astype(jnp.bfloat16)
    inner = jax.nn.relu(jnp.einsum('rsd,df->rsf', normed, w_in, preferred_element_type=jnp.float32) + b_in).astype(jnp.bfloat16)
    partial = jnp.einsum('rsf,fd->rsd', inner, w_out, preferred_element_type=jnp.float32).astype(jnp.bfloat16)
    total = lax.psum(partial, 'tp')
    return (residual.astype(jnp.float32) + total.astype(jnp.float32) + b_out).astype(jnp.bfloat16)


def route_tokens(normed_f32, key_ok, expert_idx, w_router, capacity):
    tokens = key_ok.size
    num_experts = w_router.shape[1]
    logits = jnp.dot(normed_f32.reshape(tokens, -1), w_router, preferred_element_type=jnp.float32)
    valid = key_ok.reshape(tokens)
    first = expert_idx[..., 0].reshape(tokens)
    second = expert_idx[..., 1].reshape(tokens)
    logit_first = jnp.take_along_axis(logits, first[:, None], axis=1)[:, 0]
    logit_second = jnp.take_along_axis(logits, second[:, None], axis=1)[:, 0]
    gate_first = jax.nn.sigmoid(logit_first - logit_second)
    gate_second = jax.nn.sigmoid(logit_second - logit_first)
    expert_ids = jnp.arange(num_experts, dtype=jnp.int32)
    hot_first = ((first[:, None] == expert_ids) & valid[:, None]).astype(jnp.int32)
    hot_second = ((second[:, None] == expert_ids) & valid[:, None]).astype(jnp.int32)
    rank_first = jnp.cumsum(hot_first, axis=0) - 1
    rank_second = jnp.cumsum(hot_second, axis=0) - 1 + jnp.sum(hot_first, axis=0)
    slot_first = jnp.sum(rank_first * hot_first, axis=1)
    slot_second = jnp.sum(rank_second * hot_second, axis=1)
    dump_slot = num_experts * capacity
    dest_first = jnp.where(valid & (slot_first < capacity), first * capacity + slot_first, dump_slot)
    dest_second = jnp.where(valid & (slot_second < capacity), second * capacity + slot_second, dump_slot)
    return gate_first, gate_second, dest_first, dest_second


def slot_table(dest_first, dest_second, dump_slot):
    tokens = dest_first.shape[0]
    token_ids = jnp.arange(tokens, dtype=jnp.int32)
    table = jnp.full((dump_slot + 1,), tokens, jnp.int32)
    table = table.at[dest_first].set(token_ids).at[dest_second].set(token_ids)
    return table[:dump_slot]


def solution(mesh):
    ep_size = mesh.shape['ep']

    def local_fn(x, src_len, expert_idx, ln_gain, ln_bias, w_query, b_query, w_key, w_value, b_value, w_attn_out, b_attn_out, w_fc1, b_fc1, w_fc2, b_fc2, w_router, w_exp_in, b_exp_in, w_exp_out, b_exp_out):
        rows, seq_len, d_model = x.shape
        tokens = rows * seq_len
        num_experts = w_router.shape[1]
        capacity = 2 * (-(-tokens // num_experts))
        dump_slot = num_experts * capacity
        local_experts = w_exp_in.shape[0]
        key_ok = jnp.arange(seq_len)[None, :] < src_len[:, None]
        hidden = attention_layer(x, key_ok, ln_gain[0], ln_bias[0], w_query[0], b_query[0], w_key[0], w_value[0], b_value[0], w_attn_out[0], b_attn_out[0])
        hidden = dense_ffn(hidden, ln_gain[1], ln_bias[1], w_fc1, b_fc1, w_fc2, b_fc2)
        hidden = attention_layer(hidden, key_ok, ln_gain[2], ln_bias[2], w_query[1], b_query[1], w_key[1], w_value[1], b_value[1], w_attn_out[1], b_attn_out[1])
        normed_f32 = layer_norm(hidden, ln_gain[3], ln_bias[3])
        gate_first, gate_second, dest_first, dest_second = route_tokens(normed_f32, key_ok, expert_idx, w_router, capacity)
        table = slot_table(dest_first, dest_second, dump_slot)
        padded = jnp.concatenate([normed_f32.astype(jnp.bfloat16).reshape(tokens, d_model), jnp.zeros((1, d_model), jnp.bfloat16)], axis=0)
        dispatch = padded[table].reshape(num_experts, capacity, d_model)
        received = lax.all_to_all(dispatch, 'ep', 0, 0, tiled=True).reshape(ep_size, local_experts, capacity, d_model)
        inner = jax.nn.relu(jnp.einsum('gecd,edf->gecf', received, w_exp_in, preferred_element_type=jnp.float32) + b_exp_in[None, :, None, :]).astype(jnp.bfloat16)
        partial = jnp.einsum('gecf,efd->gecd', inner, w_exp_out, preferred_element_type=jnp.float32).astype(jnp.bfloat16)
        summed = lax.psum(partial, 'tp')
        expert_out = (summed.astype(jnp.float32) + b_exp_out[None, :, None, :]).astype(jnp.bfloat16)
        returned = lax.all_to_all(expert_out.reshape(num_experts, capacity, d_model), 'ep', 0, 0, tiled=True)
        flat = jnp.concatenate([returned.reshape(dump_slot, d_model), jnp.zeros((1, d_model), jnp.bfloat16)], axis=0)
        combined = gate_first[:, None] * flat[dest_first].astype(jnp.float32) + gate_second[:, None] * flat[dest_second].astype(jnp.float32)
        result = hidden.reshape(tokens, d_model).astype(jnp.float32) + combined
        return result.astype(jnp.bfloat16).reshape(rows, seq_len, d_model)

    in_specs = (P(('dp', 'ep'), None, None), P(('dp', 'ep')), P(('dp', 'ep'), None, None), P(), P(), P(None, None, 'tp', None), P(None, 'tp', None), P(None, None, 'tp', None), P(None, None, 'tp', None), P(None, 'tp', None), P(None, 'tp', None, None), P(), P(None, 'tp'), P('tp'), P('tp', None), P(), P(), P('ep', None, 'tp'), P('ep', 'tp'), P('ep', 'tp', None), P('ep', None))
    return jax.shard_map(local_fn, mesh=mesh, in_specs=in_specs, out_specs=P(('dp', 'ep'), None, None), check_vma=False)
```

profile of v0, /device:TPU:97, one launch (start us, length us, event | category | flops | bytes accessed | tf_op | source)
XLA Modules:
  0.0 2315.1 jit_solution(7250749386747031469)
XLA Ops:
  24.5 11.7 convolution_convert_fusion.1
  36.3 8.8 fusion.113
  53.6 41.4 %fusion.157 = (f32[8,3,1024]{2,1,0:T(4,128)S(1)}, f32[8,3,1024,1024]{2,3,1,0:T(8,128)}) fusion(pred[8,1024]{1,0:T(8,128)(4,1)S(1)} %get-tuple-element.42, bf16[8,1024,3,64]{1,3,2,0:T(8,128)(2,1)} %add_convert_fusion.3, bf16[8,1024,3,64]{1,3,2,0:T(8,128)(2,1)} %convolution_convert_fusion.1), kind=kOutput, calls=%fused_computation.220 | convolution fusion | flops 3321889792 | bytes 107061248 | tf_op jit(solution)/shard_map/sub | solution.py:23
  95.0 35.3 %fusion.191 = bf16[8,1024,3,64]{1,3,2,0:T(8,128)(2,1)} fusion(f32[8,3,1024,1024]{2,3,1,0:T(8,128)} %get-tuple-element.44, f32[8,3,1024]{2,1,0:T(4,128)S(1)} %get-tuple-element.43, f32[8,1024,3,64]{1,3,2,0:T(8,128)} %fusion.113, f32[3,64]{1,0:T(4,128)S(1)} %bitcast.242), kind=kOutput, calls=%fused_computation.102.clone.2 | convolution fusion | flops 3276275712 | bytes 110199552 | tf_op jit(solution)/shard_map/rhqs,rshk->rqhk/dot_general | solution.py:24
  130.4 10.2 bitcast_convert_fusion.1
  141.3 225.8 %all-reduce.7.cloned.1.call-done = bf16[8,1024,768]{2,1,0:T(8,128)(2,1)} async-done(((bf16[8,1024,768]{2,1,0:T(8,128)(2,1)}), bf16[8,1024,768]{2,1,0:T(8,128)(2,1)}) %all-reduce.7.cloned.1.call-update) | async-done | bytes 12582928 | tf_op jit(solution)/shard_map/psum | solution.py:26
  367.2 15.9 convert_reduce_fusion.2
  391.3 25.7 %fusion.77 = bf16[8,1024,768]{2,1,0:T(8,128)(2,1)} fusion(bf16[8,1024,768]{2,1,0:T(8,128)(2,1)} %get-tuple-element.25, f32[768]{0:T(1024)S(1)} %copy-done.50, f32[768]{0:T(1024)S(1)} %copy-done.36, f32[768]{0:T(1024)S(1)} %copy-done.37, f32[8,1024]{1,0:T(8,128)S(1)} %add_rsqrt_fusion.2, f32[8,1024]{1,0:T(8,128)S(1)} %broadcast_multiply_fusion.2, ...), kind=kOutput, calls=%fused_computation.94 | convolution fusion | flops 19390267392 | bytes 27599872 | tf_op jit(solution)/shard_map/rsf,fd->rsd/dot_general | solution.py:33
  417.1 222.6 %all-reduce.9.cloned.1.call-done = bf16[8,1024,768]{2,1,0:T(8,128)(2,1)} async-done(((bf16[8,1024,768]{2,1,0:T(8,128)(2,1)}), bf16[8,1024,768]{2,1,0:T(8,128)(2,1)}) %all-reduce.9.cloned.1.call-update) | async-done | bytes 12582928 | tf_op jit(solution)/shard_map/psum | solution.py:34
  639.7 16.0 convert_reduce_fusion.1
  663.9 12.0 convolution_convert_fusion
  676.0 8.8 fusion.108
  692.7 41.6 %fusion.158 = (f32[8,3,1024]{2,1,0:T(4,128)S(1)}, f32[8,3,1024,1024]{2,3,1,0:T(8,128)}) fusion(pred[8,1024]{1,0:T(8,128)(4,1)S(1)} %copy-done.29, bf16[8,1024,3,64]{1,3,2,0:T(8,128)(2,1)} %add_convert_fusion.1, bf16[8,1024,3,64]{1,3,2,0:T(8,128)(2,1)} %convolution_convert_fusion), kind=kOutput, calls=%fused_computation.221 | convolution fusion | flops 3321889792 | bytes 107061248 | tf_op jit(solution)/shard_map/sub | solution.py:23
  734.3 33.9 %fusion.189 = bf16[8,1024,3,64]{1,3,2,0:T(8,128)(2,1)S(1)} fusion(f32[8,3,1024,1024]{2,3,1,0:T(8,128)} %get-tuple-element.46, f32[8,3,1024]{2,1,0:T(4,128)S(1)} %get-tuple-element.45, f32[8,1024,3,64]{1,3,2,0:T(8,128)} %fusion.108, f32[3,64]{1,0:T(4,128)S(1)} %bitcast.239), kind=kOutput, calls=%fused_computation.101.clone.2 | convolution fusion | flops 3276275712 | bytes 110199552 | tf_op jit(solution)/shard_map/rhqs,rshk->rqhk/dot_general | solution.py:24
  775.5 9.7 reduce-window.16
  786.4 9.5 reduce-window.14
  800.5 30.5 %scatter_custom_fusion = s32[16385]{0:T(1024)S(1)} fusion(s32[8192]{0:T(1024)S(1)} %bitcast.231, s32[8192]{0:T(1024)S(1)} %iota.26, s32[]{:T(128)} %constant.56.clone.1), kind=kCustom, calls=%fused_computation.166 | custom fusion | bytes 65544 | tf_op jit(solution)/shard_map/scatter | solution.py:66
  831.0 30.5 %scatter_fusion = s32[16385]{0:T(1024)S(1)} fusion(s32[16385]{0:T(1024)S(1)} %scatter_custom_fusion, s32[8192]{0:T(1024)S(1)} %bitcast.226, s32[8192]{0:T(1024)S(1)} %iota.27), kind=kCustom, calls=%fused_computation.6 | custom fusion | bytes 131072 | tf_op jit(solution)/shard_map/scatter | solution.py:66
  861.5 136.1 %all-reduce.11.cloned.1.call-done = bf16[8,1024,768]{2,1,0:T(8,128)(2,1)} async-done(((bf16[8,1024,768]{2,1,0:T(8,128)(2,1)}), bf16[8,1024,768]{2,1,0:T(8,128)(2,1)}) %all-reduce.11.cloned.1.call-update) | async-done | bytes 12582928 | tf_op jit(solution)/shard_map/psum | solution.py:26
  997.6 15.8 convert_reduce_fusion
  1035.4 79.3 %gather_fusion = bf16[16384,768]{1,0:T(8,128)(2,1)} fusion(bf16[8193,768]{1,0:T(8,128)(2,1)} %concatenate.6, s32[16384]{0:T(1024)S(1)} %fusion.126), kind=kCustom, calls=%fused_computation.2 | custom fusion | bytes 50397184 | tf_op jit(solution)/shard_map/gather | solution.py:88
  1114.7 284.1 %all_to_all.10 = bf16[32,512,768]{2,1,0:T(8,128)(2,1)} all-to-all(bf16[32,512,768]{2,1,0:T(8,128)(2,1)} %bitcast.210), channel_id=1, replica_groups=mesh['dp'=1,'tp'=4,'ep'=8] {'ep'}, dimensions={0} | all-to-all | bytes 50331648 | tf_op jit(solution)/shard_map/all_to_all | solution.py:89
  1398.8 47.2 %convert_bitcast_fusion = bf16[8,4,512,768]{3,2,0,1:T(8,128)(2,1)} fusion(bf16[8,4,512,768]{3,2,1,0:T(8,128)(2,1)} %bitcast.215, f32[4,768]{1,0:T(4,128)S(1)} %copy-done.49, bf16[4,768,768]{2,1,0:T(8,128)(2,1)} %param.42, bf16[4,768,768]{2,1,0:T(8,128)(2,1)} %param.40), kind=kOutput, calls=%fused_computation.78 | convolution fusion | flops 38705037312 | bytes 59781120 | tf_op jit(solution)/shard_map/gecf,efd->gecd/dot_general | solution.py:91
  1446.1 423.3 %all-reduce.13.cloned.1.call-done = bf16[8,4,512,768]{3,2,0,1:T(8,128)(2,1)} async-done(((bf16[8,4,512,768]{3,2,0,1:T(8,128)(2,1)}), bf16[8,4,512,768]{3,2,0,1:T(8,128)(2,1)}) %all-reduce.13.cloned.1.call-update) | async-done | bytes 25165840 | tf_op jit(solution)/shard_map/psum | solution.py:92
  1869.3 13.1 add_convert_fusion
  1911.7 65.6 %gather_fusion.3 = f32[8192]{0:T(1024)S(1)} fusion(f32[8192,32]{0,1:T(8,128)S(1)} %fusion.159, s32[8192]{0:T(1024)S(1)} %bitcast.204), kind=kCustom, calls=%fused_computation.clone | custom fusion | bytes 131072 | tf_op jit(solution)/shard_map/jit(take_along_axis)/gather | solution.py:45
  1977.2 65.5 %gather_fusion.4 = f32[8192]{0:T(1024)S(1)} fusion(f32[8192,32]{0,1:T(8,128)S(1)} %fusion.159, s32[8192]{0:T(1024)S(1)} %bitcast.203), kind=kCustom, calls=%fused_computation.1.clone | custom fusion | bytes 131072 | tf_op jit(solution)/shard_map/jit(take_along_axis)/gather | solution.py:46
  2043.2 129.0 %all-to-all-done.1 = bf16[32,512,768]{2,1,0:T(8,128)(2,1)} async-done(((bf16[32,512,768]{2,1,0:T(8,128)(2,1)}), bf16[32,512,768]{2,1,0:T(8,128)(2,1)}, u32[]{:S(2)}, u32[]{:S(2)}) %all-to-all-start.1) | async-done | bytes 25165856 | tf_op jit(solution)/shard_map/all_to_all | solution.py:94
  2172.2 20.5 concatenate.7
  2192.7 48.6 %gather_fusion.2 = bf16[8192,768]{1,0:T(8,128)(2,1)} fusion(bf16[16385,768]{1,0:T(8,128)(2,1)} %concatenate.7, s32[8192]{0:T(1024)S(1)} %broadcast_clamp_fusion), kind=kCustom, calls=%fused_computation.4 | custom fusion | bytes 25198592 | tf_op jit(solution)/shard_map/gather | solution.py:96
  2241.3 48.7 %gather_fusion.1 = bf16[8192,768]{1,0:T(8,128)(2,1)} fusion(bf16[16385,768]{1,0:T(8,128)(2,1)} %concatenate.7, s32[8192]{0:T(1024)S(1)} %broadcast_clamp_fusion.1), kind=kCustom, calls=%fused_computation.3 | custom fusion | bytes 25198592 | tf_op jit(solution)/shard_map/gather | solution.py:96
  2289.9 18.4 fusion.41
  (184 shorter events, 115.7 us)
Async XLA Ops:
  6.5 384.6 %copy-start = (bf16[768,768]{1,0:T(8,128)(2,1)S(1)}, bf16[768,768]{1,0:T(8,128)(2,1)}, u32[]{:S(2)}) copy-start(bf16[768,768]{1,0:T(8,128)(2,1)} %param.37) | copy-start | bytes 3538948
  6.6 360.6 %all-reduce.7.cloned.1.call-start = ((), (), s32[]{:S(2)}) async-start(), calls=%async_computation.2 | async-start | bytes 25165824 | tf_op jit(solution)/shard_map/psum | solution.py:26
  8.1 45.5 %copy-start.28 = (pred[8,1024]{1,0:T(8,128)(4,1)}, pred[8,1024]{1,0:T(8,128)(4,1)S(1)}, u32[]{:S(2)}) copy-start(pred[8,1024]{1,0:T(8,128)(4,1)S(1)} %get-tuple-element.42) | copy-start | bytes 24580
  95.0 35.3 %copy-start.47 = (bf16[2,3,64,768]{3,2,1,0:T(8,128)(2,1)S(1)}, bf16[2,3,64,768]{3,2,1,0:T(8,128)(2,1)}, u32[]{:S(2)}) copy-start(bf16[2,3,64,768]{3,2,1,0:T(8,128)(2,1)} %param.33) | copy-start | bytes 1769476
  140.6 499.1 %all-reduce.9.cloned.1.call-start = ((), (), s32[]{:S(2)}) async-start(), calls=%async_computation.3 | async-start | bytes 25165824 | tf_op jit(solution)/shard_map/psum | solution.py:34
  367.1 24.1 %copy-start.36 = (f32[768]{0:T(1024)S(1)}, f32[768]{0:T(1024)}, u32[]{:S(2)}) copy-start(f32[768]{0:T(1024)} %get-tuple-element.15) | copy-start | bytes 9220
  367.1 24.1 %copy-start.37 = (f32[768]{0:T(1024)S(1)}, f32[768]{0:T(1024)}, u32[]{:S(2)}) copy-start(f32[768]{0:T(1024)} %get-tuple-element.49) | copy-start | bytes 9220
  367.2 24.1 %copy-start.40 = (bf16[768,768]{1,0:T(8,128)(2,1)S(1)}, bf16[768,768]{1,0:T(8,128)(2,1)}, u32[]{:S(2)}) copy-start(bf16[768,768]{1,0:T(8,128)(2,1)} %param.35) | copy-start | bytes 3538948
  367.2 24.1 %copy-start.50 = (f32[768]{0:T(1024)S(1)}, f32[768]{0:T(1024)}, u32[]{:S(2)}) copy-start(f32[768]{0:T(1024)} %param.36) | copy-start | bytes 9220
  391.2 25.8 %copy-start.31 = (f32[1,3,64]{2,0,1:T(1,128)S(1)}, f32[1,3,64]{2,0,1:T(1,128)}, u32[]{:S(2)}) copy-start(f32[1,3,64]{2,0,1:T(1,128)} %get-tuple-element.39) | copy-start | bytes 2308
  391.3 25.8 %copy-start.32 = (f32[1,3,64]{2,0,1:T(1,128)S(1)}, f32[1,3,64]{2,0,1:T(1,128)}, u32[]{:S(2)}) copy-start(f32[1,3,64]{2,0,1:T(1,128)} %get-tuple-element.36) | copy-start | bytes 2308
  391.3 248.5 %copy-start.33 = (f32[768]{0:T(1024)S(1)}, f32[768]{0:T(1024)}, u32[]{:S(2)}) copy-start(f32[768]{0:T(1024)} %param.38) | copy-start | bytes 9220
  417.0 580.6 %all-reduce.11.cloned.1.call-start = ((), (), s32[]{:S(2)}) async-start(), calls=%async_computation.4 | async-start | bytes 25165824 | tf_op jit(solution)/shard_map/psum | solution.py:26
  417.1 246.8 %copy-start.34 = (f32[768]{0:T(1024)S(1)}, f32[768]{0:T(1024)}, u32[]{:S(2)}) copy-start(f32[768]{0:T(1024)} %get-tuple-element.17) | copy-start | bytes 9220
  417.1 246.8 %copy-start.35 = (f32[768]{0:T(1024)S(1)}, f32[768]{0:T(1024)}, u32[]{:S(2)}) copy-start(f32[768]{0:T(1024)} %get-tuple-element.47) | copy-start | bytes 9220
  417.1 246.8 %copy-start.42 = (bf16[2,768,3,64]{1,3,2,0:T(8,128)(2,1)S(1)}, bf16[2,768,3,64]{1,3,2,0:T(8,128)(2,1)}, u32[]{:S(2)}) copy-start(bf16[2,768,3,64]{1,3,2,0:T(8,128)(2,1)} %param.30) | copy-start | bytes 1769476
  734.3 33.9 %copy-start.48 = (bf16[2,3,64,768]{3,2,1,0:T(8,128)(2,1)S(1)}, bf16[2,3,64,768]{3,2,1,0:T(8,128)(2,1)}, u32[]{:S(2)}) copy-start(bf16[2,3,64,768]{3,2,1,0:T(8,128)(2,1)} %param.33) | copy-start | bytes 1769476
  768.3 28.8 %copy-start.22 = (pred[1,1,8,1024]{3,2,1,0:T(8,128)(4,1)S(1)}, pred[1,1,8,1024]{3,2,1,0:T(8,128)(4,1)}, u32[]{:S(2)}) copy-start(pred[1,1,8,1024]{3,2,1,0:T(8,128)(4,1)} %get-tuple-element.40) | copy-start | bytes 24580
  774.8 1094.5 %all-reduce.13.cloned.1.call-start = ((), (), s32[]{:S(2)}) async-start(), calls=%async_computation.5 | async-start | bytes 50331648 | tf_op jit(solution)/shard_map/psum | solution.py:92
  775.2 86.2 %copy-start.2 = (s32[8,1024,1]{1,2,0:T(1,128)}, s32[8,1024,1]{1,2,0:T(1,128)S(1)}, u32[]{:S(2)}) copy-start(s32[8,1024,1]{1,2,0:T(1,128)S(1)} %get-tuple-element.26) | copy-start | bytes 98308
  775.2 86.2 %copy-start.4 = (s32[8,1024,1]{1,2,0:T(1,128)}, s32[8,1024,1]{1,2,0:T(1,128)S(1)}, u32[]{:S(2)}) copy-start(s32[8,1024,1]{1,2,0:T(1,128)S(1)} %get-tuple-element.27) | copy-start | bytes 98308
  800.5 30.5 %copy-start.14 = (s32[8192,1]{0,1:T(1,128)}, s32[8192,1]{0,1:T(1,128)S(1)}, u32[]{:S(2)}) copy-start(s32[8192,1]{0,1:T(1,128)S(1)} %get-tuple-element.32) | copy-start | bytes 98308
  800.5 61.0 %copy-start.8 = (s32[8192,1]{0,1:T(1,128)}, s32[8192,1]{0,1:T(1,128)S(1)}, u32[]{:S(2)}) copy-start(s32[8192,1]{0,1:T(1,128)S(1)} %get-tuple-element.31) | copy-start | bytes 98308
  831.0 166.6 %copy-start.24 = (f32[768]{0:T(1024)S(1)}, f32[768]{0:T(1024)}, u32[]{:S(2)}) copy-start(f32[768]{0:T(1024)} %get-tuple-element.18) | copy-start | bytes 9220
  997.6 24.0 %copy-start.18 = (f32[768]{0:T(1024)S(1)}, f32[768]{0:T(1024)}, u32[]{:S(2)}) copy-start(f32[768]{0:T(1024)} %get-tuple-element.14) | copy-start | bytes 9220
  997.6 24.0 %copy-start.20 = (f32[768]{0:T(1024)S(1)}, f32[768]{0:T(1024)}, u32[]{:S(2)}) copy-start(f32[768]{0:T(1024)} %get-tuple-element.50) | copy-start | bytes 9220
  1013.5 21.9 copy-start.6
  1114.7 284.1 %copy-start.49 = (f32[4,768]{1,0:T(4,128)S(1)}, f32[4,768]{1,0:T(4,128)}, u32[]{:S(2)}) copy-start(f32[4,768]{1,0:T(4,128)} %param.41) | copy-start | bytes 36868
  1446.0 423.3 %copy-start.25 = (f32[4,768]{1,0:T(4,128)S(1)}, f32[4,768]{1,0:T(4,128)}, u32[]{:S(2)}) copy-start(f32[4,768]{1,0:T(4,128)} %param.43) | copy-start | bytes 36868
  1891.1 281.1 %all-to-all-start.1 = ((bf16[32,512,768]{2,1,0:T(8,128)(2,1)}), bf16[32,512,768]{2,1,0:T(8,128)(2,1)}, u32[]{:S(2)}, u32[]{:S(2)}) async-start(bf16[32,512,768]{2,1,0:T(8,128)(2,1)} %bitcast.209), calls=%async_computation.1 | async-start | bytes 50331648 | tf_op jit(solution)/shard_map/all_to_all | solution.py:94
  1977.2 65.6 %copy-start.3 = (s32[8,1024,1]{1,2,0:T(1,128)S(1)}, s32[8,1024,1]{1,2,0:T(1,128)}, u32[]{:S(2)}) copy-start(s32[8,1024,1]{1,2,0:T(1,128)} %copy-done.2) | copy-start | bytes 98308
  1977.2 65.6 %copy-start.5 = (s32[8,1024,1]{1,2,0:T(1,128)S(1)}, s32[8,1024,1]{1,2,0:T(1,128)}, u32[]{:S(2)}) copy-start(s32[8,1024,1]{1,2,0:T(1,128)} %copy-done.4) | copy-start | bytes 98308
  (30 other events, 332.3 us)
Sparse Core Ops, SparseCore 0:
  140.8 226.3 all-reduce.6
  417.1 222.5 all-reduce.8
  774.9 222.6 all-reduce.10
  1446.2 423.0 all-reduce.12
where the time goes:
time: 2320 us
  waiting for transfers between devices  1140 us (49%)
  local copies, waits for them, and re-layouts  408 us (18%)
  matrix products  303 us (13%)
  blocking collectives  284 us (12%)
  other arithmetic  161 us (7%)
    psum x1, waiting for transfers between devices, local_fn(): summed = lax.psum(partial, 'tp')  423 us
    psum x2, waiting for transfers between devices, attention_layer(): total = lax.psum(partial, 'tp')  362 us
    all_to_all x1, blocking collectives, local_fn(): lax.all_to_all(dispatch, 'ep', 0, 0, tiled=True)  284 us
    psum x1, waiting for transfers between devices, dense_ffn(): total = lax.psum(partial, 'tp')  223 us
    all_to_all x1, waiting for transfers between devices, local_fn(): lax.all_to_all(expert_out.reshape(num_experts, capacity, d_model), 'ep',...  129 us
    sub x2, matrix products, attention_layer(): attn_probs = jax.nn.softmax(scores, axis=-1).astype(jnp.bfloat16)  83 us
    gather x1, local copies, waits for them, and re-layouts, local_fn(): dispatch = padded[table].reshape(num_experts, capacity, d_model)  79.3 us
    dot_general x2, matrix products, attention_layer(): jnp.einsum('rhqs,rshk->rqhk', attn_probs, values, preferred_element_type=...  69.2 us
  transfers between devices with their start and end apart: 5, of which 5 were waited for; matrix products, arithmetic and copies ran while one was open for 10% of the time, Pallas kernels for 0%

commit v1 on v0

v1 whole, which is shorter than its diff:
```python
import functools

import jax
import jax.numpy as jnp
from jax import lax
from jax.experimental import pallas as pl
from jax.experimental.pallas import tpu as pltpu
from jax.sharding import PartitionSpec as P

LN_EPS = 1e-5
LOG2_E = 1.4426950408889634
UNROLL = 4


def layer_norm(hidden, gain, shift):
    hidden = hidden.astype(jnp.float32)
    centered = hidden - jnp.mean(hidden, axis=-1, keepdims=True)
    variance = jnp.mean(centered * centered, axis=-1, keepdims=True)
    return centered * lax.rsqrt(variance + LN_EPS) * gain + shift


def dot_rows(lhs, rhs):
    return lax.dot_general(lhs, rhs, (((1,), (0,)), ((), ())), preferred_element_type=jnp.float32)


def dot_cols(lhs, rhs):
    return lax.dot_general(lhs, rhs, (((1,), (1,)), ((), ())), preferred_element_type=jnp.float32)


def attention_kernel(head_dim, q_block, len_ref, q_ref, k_ref, v_ref, o_ref):
    seq, lanes = k_ref.shape
    real_keys = len_ref[pl.program_id(0)]
    scale = head_dim ** -0.5 * LOG2_E
    lane = lax.broadcasted_iota(jnp.int32, (1, lanes), 1)
    key_lane = lax.broadcasted_iota(jnp.int32, (seq, lanes), 1)
    key_ok = lax.broadcasted_iota(jnp.int32, (seq, lanes), 0) < real_keys
    pad_bias = jnp.where(key_ok, 0.0, -1e30)
    keys_f32 = k_ref[...].astype(jnp.float32)
    values = v_ref[...]
    heads = []
    for head in range(lanes // head_dim):
        spare = (head + 1) * head_dim % lanes
        own = (key_lane // head_dim == head) & key_ok
        heads.append((jnp.where(own, keys_f32, jnp.where(key_lane == spare, pad_bias, 0.0)).astype(jnp.bfloat16), spare))

    def block(i, carry):
        rows = pl.ds(pl.multiple_of(i * q_block, q_block), q_block)
        q_all = q_ref[rows, :].astype(jnp.float32)
        result = jnp.zeros((q_block, lanes), jnp.float32)
        for head, (keys, spare) in enumerate(heads):
            own = lane // head_dim == head
            query = jnp.where(own, q_all, jnp.where(lane == spare, 1.0, 0.0)).astype(jnp.bfloat16)
            scores = dot_cols(query, keys)
            top = jnp.max(scores, axis=-1, keepdims=True)
            weights = jnp.exp2((scores - top) * scale)
            total = jnp.sum(weights, axis=-1, keepdims=True)
            probs = (weights * (1.0 / total)).astype(jnp.bfloat16)
            result = jnp.where(own, dot_rows(probs, values), result)
        o_ref[rows, :] = result.astype(jnp.bfloat16)
        return carry

    lax.fori_loop(0, seq // q_block, block, 0, unroll=UNROLL)


def attend(query, keys, values, src_len, seq, head_dim):
    tokens, width = query.shape
    rows = tokens // seq
    lanes = 128
    spec = pl.BlockSpec((seq, lanes), lambda r, c, lens: (r, c))
    heads = width // head_dim
    return pl.pallas_call(
        functools.partial(attention_kernel, head_dim, 256),
        out_shape=jax.ShapeDtypeStruct((tokens, width), jnp.bfloat16),
        grid_spec=pltpu.PrefetchScalarGridSpec(num_scalar_prefetch=1, grid=(rows, width // lanes), in_specs=[spec, spec, spec], out_specs=spec),
        compiler_params=pltpu.CompilerParams(dimension_semantics=('arbitrary', 'arbitrary')),
        cost_estimate=pl.CostEstimate(flops=40 * rows * heads * seq * seq * head_dim, bytes_accessed=8 * tokens * width, transcendentals=rows * heads * seq * seq),
        name='attend',
    )(src_len, query, keys, values)


def attention_layer(residual, normed, src_len, seq, head_dim, w_q, b_q, w_k, w_v, b_v, w_o, b_o):
    query = (dot_cols(normed, w_q) + b_q).astype(jnp.bfloat16)
    keys = dot_cols(normed, w_k).astype(jnp.bfloat16)
    values = (dot_cols(normed, w_v) + b_v).astype(jnp.bfloat16)
    context = attend(query, keys, values, src_len, seq, head_dim)
    return (residual.astype(jnp.float32) + dot_rows(context, w_o) + b_o).astype(jnp.bfloat16)


def dense_ffn(residual, gain, shift, blocks, b_out):
    normed = layer_norm(residual, gain, shift).astype(jnp.bfloat16)
    projected = 0.0
    for w_in, b_in, w_out in blocks:
        inner = jax.nn.relu(dot_cols(normed, w_in) + b_in).astype(jnp.bfloat16)
        projected = projected + dot_rows(inner, w_out)
    return (residual.astype(jnp.float32) + projected + b_out).astype(jnp.bfloat16)


def route_slots(valid, first, second, num_experts, capacity):
    expert_ids = jnp.arange(num_experts, dtype=jnp.int32)
    hot_first = ((first[:, None] == expert_ids) & valid[:, None]).astype(jnp.int32)
    hot_second = ((second[:, None] == expert_ids) & valid[:, None]).astype(jnp.int32)
    rank_first = jnp.cumsum(hot_first, axis=0) - 1
    rank_second = jnp.cumsum(hot_second, axis=0) - 1 + jnp.sum(hot_first, axis=0)
    slot_first = jnp.sum(rank_first * hot_first, axis=1)
    slot_second = jnp.sum(rank_second * hot_second, axis=1)
    return slot_first, slot_second, valid & (slot_first < capacity), valid & (slot_second < capacity)


def solution(mesh):
    ep_size = mesh.shape['ep']
    tp_size = mesh.shape['tp']

    def gathered(shard):
        return lax.all_gather(shard, 'tp', axis=0, tiled=True)

    def local_fn(x, src_len, expert_idx, ln_gain, ln_bias, w_query, b_query, w_key, w_value, b_value, w_attn_out, b_attn_out, w_fc1, b_fc1, w_fc2, b_fc2, w_router, w_exp_in, b_exp_in, w_exp_out, b_exp_out):
        rows, seq_len, d_model = x.shape
        tokens = rows * seq_len
        num_experts = w_router.shape[1]
        capacity = 2 * (-(-tokens // num_experts))
        local_experts = w_exp_in.shape[0]
        layers, _, local_heads, head_dim = w_query.shape
        head_width = local_heads * head_dim
        part = capacity // tp_size
        own_rows = rows // tp_size
        me = lax.axis_index('tp')

        def whole(parts, height):
            return lax.all_gather(jnp.concatenate([w.reshape(-1, height, d_model) for w in parts], axis=0), 'tp', axis=1, tiled=True)

        def cols(w):
            return w.reshape(d_model, head_width).T

        biases = jnp.concatenate([b_query.reshape(-1), b_value.reshape(-1), b_fc1, b_exp_in.reshape(-1)])
        biases = lax.all_gather(biases, 'tp', axis=0)
        sizes = [layers * head_width, layers * head_width, b_fc1.shape[0], b_exp_in.size]
        offsets = [sum(sizes[:i]) for i in range(5)]
        b_q, b_v, b_in, b_expert = [biases[:, offsets[i]:offsets[i + 1]] for i in range(4)]
        b_q = b_q.reshape(tp_size, layers, head_width).transpose(1, 0, 2).reshape(layers, -1)
        b_v = b_v.reshape(tp_size, layers, head_width).transpose(1, 0, 2).reshape(layers, -1)
        b_expert = b_expert.reshape(tp_size, local_experts, -1).transpose(1, 0, 2).reshape(local_experts, -1)

        ep_me = lax.axis_index('ep')
        slab = w_fc1.shape[1] // ep_size
        slab_in = lax.dynamic_slice_in_dim(w_fc1, ep_me * slab, slab, 1).T
        slab_out = lax.dynamic_slice_in_dim(w_fc2, ep_me * slab, slab, 0)
        mine, choices = lax.optimization_barrier((whole([slab_in, slab_out], slab), expert_idx))
        cores = 2
        parts, owners = [mine], [ep_me]
        for step in range(cores, ep_size, cores):
            parts.append(lax.ppermute(mine, 'ep', [(e, (e + step) % ep_size) for e in range(ep_size)]))
            owners.append((ep_me + ep_size - step) % ep_size)
        core_half = jnp.concatenate(parts, axis=1)
        other_half = lax.ppermute(core_half, 'ep', [(e, e ^ 1) for e in range(ep_size)])
        owners = jnp.stack(owners)
        b_slabs = b_in.reshape(tp_size, ep_size, slab).transpose(1, 0, 2)

        def slab_bias(e):
            return jnp.sum(jnp.where((e[:, None] == jnp.arange(ep_size))[:, :, None, None], b_slabs[None], 0.0), axis=1).reshape(-1)

        sibling = ep_me + 1 - 2 * (ep_me % cores)
        other_owners = jnp.stack([(sibling + ep_size - step) % ep_size for step in range(0, ep_size, cores)])

        qkvo = whole([cols(w_query[0]), cols(w_key[0]), cols(w_value[0]), w_attn_out[0]], head_width)
        later = whole([cols(w_query[1]), cols(w_key[1]), cols(w_value[1]), w_attn_out[1]], head_width)
        second_weights = later[0], later[1], later[2], later[3]
        ff_part = w_exp_in.shape[2]

        def expert_weights(experts, after):
            parts, after = lax.optimization_barrier(([w for e in experts for w in (w_exp_in[e].T, w_exp_out[e])], after))
            both = whole(parts, ff_part)
            return [(both[2 * i], both[2 * i + 1]) for i in range(len(experts))], after


        dense_blocks = [(core_half[0], slab_bias(owners), core_half[1]), (other_half[0], slab_bias(other_owners), other_half[1])]
        first_weights = qkvo[0], qkvo[1], qkvo[2], qkvo[3]

        own_x = lax.dynamic_index_in_dim(x.reshape(own_rows, tp_size, seq_len, d_model), me, 1, keepdims=False).reshape(own_rows * seq_len, d_model)
        own_len = lax.dynamic_index_in_dim(src_len.reshape(own_rows, tp_size), me, 1, keepdims=False)

        def norm(v, i):
            return layer_norm(v, ln_gain[i], ln_bias[i]).astype(jnp.bfloat16)

        def attention(v, normed, lens, j, weights):
            w_q, w_k, w_v, w_o = weights
            return attention_layer(v, normed, lens, seq_len, head_dim, w_q, b_q[j], w_k, w_v, b_v[j], w_o, b_attn_out[j])

        expert_w, own_normed = expert_weights(list(range(local_experts // 2)), norm(own_x, 0))
        key_ok = jnp.arange(seq_len)[None, :] < src_len[:, None]
        valid = key_ok.reshape(tokens)
        first = choices[..., 0].reshape(tokens)
        second = choices[..., 1].reshape(tokens)
        slot_first, slot_second, keep_first, keep_second = route_slots(valid, first, second, num_experts, capacity)
        dump_slot = num_experts * capacity
        token_ids = jnp.arange(tokens, dtype=jnp.int32)
        table = jnp.zeros((dump_slot + 1,), jnp.int32)
        own_normed, slot_first, slot_second = lax.optimization_barrier((own_normed, slot_first, slot_second))
        own = attention(own_x, own_normed, own_len, 0, first_weights)
        own = dense_ffn(own, ln_gain[1], ln_bias[1], dense_blocks, b_fc2)
        chunks = []
        for c in range(own_rows):
            row = own[c * seq_len:(c + 1) * seq_len]
            out = attention(row, norm(row, 2), own_len[c:c + 1], 1, second_weights)
            if c == 0:
                out, expert_w[0] = lax.optimization_barrier((out, expert_w[0]))
            if c == own_rows - 1:
                more, out = expert_weights(list(range(local_experts // 2, local_experts)), out)
                expert_w += more
            chunks.append(gathered(out))

        table = table.at[jnp.where(keep_first, first * capacity + slot_first, dump_slot)].set(token_ids)
        table = table.at[jnp.where(keep_second, second * capacity + slot_second, dump_slot)].set(token_ids)
        table = table[:dump_slot].reshape(ep_size, local_experts, tp_size, part)
        table = lax.dynamic_index_in_dim(table, me, 2, keepdims=False)

        hidden = jnp.concatenate(chunks, axis=0)
        normed_f32 = layer_norm(hidden, ln_gain[3], ln_bias[3])
        logits = jnp.dot(normed_f32, w_router, preferred_element_type=jnp.float32)
        expert_ids = jnp.arange(num_experts, dtype=jnp.int32)
        logit_first = jnp.sum(jnp.where(first[:, None] == expert_ids, logits, 0.0), axis=1)
        logit_second = jnp.sum(jnp.where(second[:, None] == expert_ids, logits, 0.0), axis=1)
        gate_first = jax.nn.sigmoid(logit_first - logit_second)
        gate_second = jax.nn.sigmoid(logit_second - logit_first)

        normed = normed_f32.astype(jnp.bfloat16)
        returned = []
        pair = local_experts // 2
        starts = range(0, local_experts, pair)
        dispatch = [normed[table[:, start:start + pair].reshape(-1)].reshape(ep_size, pair, part, d_model) for start in starts]
        for n, start in enumerate(starts):
            received = lax.all_to_all(dispatch[n], 'ep', 0, 0, tiled=True)
            if n == 0:
                received, *dispatch[1:] = lax.optimization_barrier((received, *dispatch[1:]))
            outs = []
            for e in range(start, start + pair):
                w_in, w_out = expert_w[e]
                inner = jax.nn.relu(dot_cols(received[:, e - start].reshape(-1, d_model), w_in) + b_expert[e]).astype(jnp.bfloat16)
                outs.append((dot_rows(inner, w_out) + b_exp_out[e]).astype(jnp.bfloat16).reshape(ep_size, part, d_model))
            back = lax.all_to_all(jnp.stack(outs, axis=1), 'ep', 0, 0, tiled=True)
            returned.append(gathered(back.reshape(-1, d_model)))
        flat = jnp.concatenate(returned, axis=0)

        def place(expert, slot):
            owner, e = expert // local_experts, expert % local_experts
            return (((e // pair * tp_size + slot // part) * ep_size + owner) * pair + e % pair) * part + slot % part

        out_first = flat[jnp.where(keep_first, place(first, slot_first), 0)].astype(jnp.float32)
        out_second = flat[jnp.where(keep_second, place(second, slot_second), 0)].astype(jnp.float32)
        combined = jnp.where(keep_first[:, None], gate_first[:, None] * out_first, 0.0) + jnp.where(keep_second[:, None], gate_second[:, None] * out_second, 0.0)
        return (hidden.astype(jnp.float32) + combined).astype(jnp.bfloat16).reshape(rows, seq_len, d_model)

    in_specs = (P(('dp', 'ep'), None, None), P(('dp', 'ep')), P(('dp', 'ep'), None, None), P(), P(), P(None, None, 'tp', None), P(None, 'tp', None), P(None, None, 'tp', None), P(None, None, 'tp', None), P(None, 'tp', None), P(None, 'tp', None, None), P(), P(None, 'tp'), P('tp'), P('tp', None), P(), P(), P('ep', None, 'tp'), P('ep', 'tp'), P('ep', 'tp', None), P('ep', None))
    return jax.shard_map(local_fn, mesh=mesh, in_specs=in_specs, out_specs=P(('dp', 'ep'), None, None), check_vma=False)
```

time: 2320 us -> 1000 us (0.43)
  waiting for transfers between devices: 1140 us -> 110 us
  matrix products: 303 us -> 157 us
  blocking collectives: 284 us -> 139 us
  Pallas kernels: 0 us -> 131 us
  local copies, waits for them, and re-layouts: 408 us -> 320 us
  other arithmetic: 161 us -> 114 us
    psum x4 -> x0, waiting for transfers between devices: 1010 us -> none  [the longest x1 423 us: local_fn(): summed = lax.psum(partial, 'tp')]
    gather x5 -> x4, local copies, waits for them, and re-layouts: 308 us -> 130 us  [the longest x1 48.6 us: local_fn(): flat[jnp.where(keep_first, place(first, slot_first), 0)].astype(jnp.float32)]
    all_to_all x1 -> x3, blocking collectives: 284 us -> 126 us  [the longest x2 83.6 us: local_fn(): back = lax.all_to_all(jnp.stack(outs, axis=1), 'ep', 0, 0, tiled=True)]
    pallas_call x0 -> x3, Pallas kernels: none -> 131 us  [attend(): pl.pallas_call(functools.partial(attention_kernel, head_dim, 256), out_sh...]
    all_to_all x1, waiting for transfers between devices: 129 us -> 20.8 us  [local_fn(): received = lax.all_to_all(dispatch[n], 'ep', 0, 0, tiled=True)]
    sub x2 -> x0, matrix products: 83 us -> none  [attention_layer(): attn_probs = jax.nn.softmax(scores, axis=-1).astype(jnp.bfloat16)]
    dot_general x13 -> x21, matrix products: 220 us -> 157 us  [the longest x9 92.9 us: dot_rows(): lax.dot_general(lhs, rhs, (((1,), (0,)), ((), ())), preferred_element_typ...]
    all_gather x0 -> x9, waiting for transfers between devices: none -> 62.4 us  [the longest x4 62.4 us: gathered(): return lax.all_gather(shard, 'tp', axis=0, tiled=True)]
  transfers between devices with their start and end apart: 5 -> 14, of which waited for: 5 -> 4; matrix products, arithmetic and copies ran while one was open for 10% -> 46% of each run, Pallas kernels for 0% -> 13%
where the time goes in v1:
time: 1000 us; the launch traced here: 995 us
  local copies, waits for them, and re-layouts  320 us (32%)
  matrix products  157 us (16%)
  blocking collectives  139 us (14%)
  Pallas kernels  131 us (13%)
  other arithmetic  114 us (11%)
  waiting for transfers between devices  110 us (11%)
  between operations  14.5 us (1%)
  starting transfers between devices  10.4 us (1%)
    pallas_call x3, Pallas kernels, attend(): pl.pallas_call(functools.partial(attention_kernel, head_dim, 256), out_sh...  131 us
    dot_general x9, matrix products, dot_rows(): lax.dot_general(lhs, rhs, (((1,), (0,)), ((), ())), preferred_element_typ...  92.9 us
    all_to_all x2, blocking collectives, local_fn(): back = lax.all_to_all(jnp.stack(outs, axis=1), 'ep', 0, 0, tiled=True)  83.6 us
    all_gather x4, waiting for transfers between devices, gathered(): return lax.all_gather(shard, 'tp', axis=0, tiled=True)  62.4 us
    dot_general x11, matrix products, dot_cols(): lax.dot_general(lhs, rhs, (((1,), (1,)), ((), ())), preferred_element_typ...  55.1 us
    gather x1, local copies, waits for them, and re-layouts, local_fn(): flat[jnp.where(keep_first, place(first, slot_first), 0)].astype(jnp.float32)  48.6 us
    gather x1, local copies, waits for them, and re-layouts, local_fn(): flat[jnp.where(keep_second, place(second, slot_second), 0)]  48.4 us
    unnamed x142, local copies, waits for them, and re-layouts  42.5 us
  transfers between devices with their start and end apart: 14, of which 4 were waited for; matrix products, arithmetic and copies ran while one was open for 46% of the time, Pallas kernels for 13%

profile of v1, /device:TPU:97, one launch (start us, length us, event | category | flops | bytes accessed | tf_op | source)
XLA Modules:
  0.0 995.3 jit_solution(13762663287862835892)
XLA Ops:
  17.7 8.8 copy.90
  65.2 13.2 %all-gather.1 = f32[4,1,4608]{2,1,0:T(1,128)S(1)} all-gather(f32[1,1,4608]{2,1,0:T(1,128)S(1)} %reshape.558), channel_id=2, replica_groups=mesh['dp'=1,'tp'=4,'ep'=8] {'tp'}, dimensions={0}, use_global_device_ids=true | all-gather | bytes 92160 | tf_op jit(solution)/shard_map/all_gather | solution.py:135
  90.1 9.7 reduce-window.14
  101.3 9.5 reduce-window.16
  116.5 26.6 %collective-permute-done = bf16[2,384,768]{2,1,0:T(8,128)(2,1)} collective-permute-done((bf16[2,384,768]{2,1,0:T(8,128)(2,1)}, bf16[2,384,768]{2,1,0:T(8,128)(2,1)}, u32[]{:S(2)}, u32[]{:S(2)}) %collective-permute-start) | collective-permute-done | bytes 1179680 | tf_op jit(solution)/shard_map/ppermute | solution.py:151
  168.1 64.2 %attend.3 = bf16[2048,768]{1,0:T(8,128)(2,1)} custom-call(s32[2]{0:T(128)} %get-tuple-element.77.len_ref, bf16[2048,768]{1,0:T(8,128)(2,1)} %add_convert_fusion.2.q_ref, bf16[2048,768]{1,0:T(8,128)(2,1)} %convolution_convert_fusion.k_ref, bf16[2048,768]{1,0:T(8,128)(2,1)} %add_convert_fusion.1.v_ref), custom_call_target="tpu_custom_call" | custom-call | flops 64424509440 | bytes 12582912 | tf_op jit(solution)/shard_map/attend/pallas_call | solution.py:71
  248.0 8.2 maximum_convert_fusion.4
  284.1 33.3 %attend.5 = bf16[1024,768]{1,0:T(8,128)(2,1)} custom-call(s32[1]{0:T(128)} %bitcast.72.len_ref, bf16[1024,768]{1,0:T(8,128)(2,1)} %add_convert_fusion.9.q_ref, bf16[1024,768]{1,0:T(8,128)(2,1)} %convolution_convert_fusion.1.k_ref, bf16[1024,768]{1,0:T(8,128)(2,1)} %add_convert_fusion.8.v_ref), custom_call_target="tpu_custom_call" | custom-call | flops 32212254720 | bytes 6291456 | tf_op jit(solution)/shard_map/attend/pallas_call | solution.py:71
  333.6 33.4 %attend.4 = bf16[1024,768]{1,0:T(8,128)(2,1)} custom-call(s32[1]{0:T(128)} %bitcast.45.len_ref, bf16[1024,768]{1,0:T(8,128)(2,1)} %add_convert_fusion.11.q_ref, bf16[1024,768]{1,0:T(8,128)(2,1)} %convolution_convert_fusion.2.k_ref, bf16[1024,768]{1,0:T(8,128)(2,1)} %add_convert_fusion.10.v_ref), custom_call_target="tpu_custom_call" | custom-call | flops 32212254720 | bytes 6291456 | tf_op jit(solution)/shard_map/attend/pallas_call | solution.py:71
  385.5 30.5 %scatter_custom_fusion = s32[16385]{0:T(1024)S(1)} fusion(s32[8192]{0:T(1024)S(1)} %get-tuple-element.114, s32[8192]{0:T(1024)S(1)} %iota.35, s32[]{:T(128)} %constant.212.clone.1), kind=kCustom, calls=%fused_computation.192 | custom fusion | bytes 65544 | tf_op jit(solution)/shard_map/scatter | solution.py:211
  416.0 30.5 %scatter_fusion = s32[16385]{0:T(1024)S(1)} fusion(s32[16385]{0:T(1024)S(1)} %scatter_custom_fusion, s32[8192]{0:T(1024)S(1)} %get-tuple-element.113, s32[8192]{0:T(1024)S(1)} %iota.36), kind=kCustom, calls=%fused_computation.5 | custom fusion | bytes 131072 | tf_op jit(solution)/shard_map/scatter | solution.py:212
  449.3 8.7 convert_reduce_fusion
  469.0 16.7 %copy.79 = bf16[8192,768]{1,0:T(8,128)(2,1)} copy(bf16[8192,768]{0,1:T(8,128)(2,1)} %fusion.5) | data formatting | bytes 25165824 | tf_op jit(solution)/shard_map/convert_element_type | solution.py:225
  485.7 16.3 %gather_fusion = bf16[2048,768]{1,0:T(8,128)(2,1)} fusion(bf16[8192,768]{1,0:T(8,128)(2,1)} %copy.79, s32[2048]{0:T(1024)S(1)} %broadcast_clamp_fusion.1), kind=kCustom, calls=%fused_computation | custom fusion | bytes 6299648 | tf_op jit(solution)/shard_map/gather | solution.py:229
  507.5 16.4 %gather_fusion.1 = bf16[2048,768]{1,0:T(8,128)(2,1)} fusion(bf16[8192,768]{1,0:T(8,128)(2,1)} %copy.79, s32[2048]{0:T(1024)S(1)} %broadcast_clamp_fusion), kind=kCustom, calls=%fused_computation.1 | custom fusion | bytes 6299648 | tf_op jit(solution)/shard_map/gather | solution.py:229
  524.0 20.8 %all-to-all-done = bf16[8,2,128,768]{3,2,1,0:T(8,128)(2,1)} async-done(((bf16[8,2,128,768]{3,2,1,0:T(8,128)(2,1)}), bf16[8,2,128,768]{3,2,1,0:T(8,128)(2,1)}, u32[]{:S(2)}, u32[]{:S(2)}) %all-to-all-start) | async-done | bytes 3145760 | tf_op jit(solution)/shard_map/all_to_all | solution.py:231
  548.1 15.4 %add_convert_fusion.7 = bf16[1024,768]{1,0:T(8,128)(2,1)} fusion(bf16[3072,768]{1,0:T(8,128)(2,1)} %get-tuple-element.39, f32[3072]{0:T(1024)S(1)} %bitcast.355, bf16[1024,768]{1,0:T(8,128)(2,1)} %bitcast.312, bf16[3072,768]{1,0:T(8,128)(2,1)} %get-tuple-element.38, f32[768]{0:T(1024)S(1)} %get-tuple-element.57), kind=kOutput, calls=%fused_computation.100 | convolution fusion | flops 9674686464 | bytes 12598272 | tf_op jit(solution)/shard_map/dot_general | solution.py:23
  563.5 15.0 %add_convert_fusion.6 = bf16[1024,768]{1,0:T(8,128)(2,1)} fusion(bf16[4,3072,768]{2,1,0:T(8,128)(2,1)} %all-gather.18.cloned.1.call-done, f32[3072]{0:T(1024)S(1)} %bitcast.354, bf16[1024,768]{1,0:T(8,128)(2,1)S(1)} %bitcast.308, f32[768]{0:T(1024)S(1)} %get-tuple-element.56), kind=kOutput, calls=%fused_computation.99 | convolution fusion | flops 9674686464 | bytes 12598272 | tf_op jit(solution)/shard_map/dot_general | solution.py:23
  580.7 41.7 %all_to_all.20 = bf16[8,2,128,768]{3,2,1,0:T(8,128)(2,1)} all-to-all(bf16[8,2,128,768]{3,2,1,0:T(8,128)(2,1)S(1)} %pad_maximum_fusion.3), channel_id=1, replica_groups=mesh['dp'=1,'tp'=4,'ep'=8] {'ep'}, dimensions={0} | all-to-all | bytes 6291456 | tf_op jit(solution)/shard_map/all_to_all | solution.py:239
  622.5 42.0 %all_to_all.21 = bf16[8,2,128,768]{3,2,1,0:T(8,128)(2,1)S(1)} all-to-all(bf16[8,2,128,768]{3,2,1,0:T(8,128)(2,1)} %bitcast.293), channel_id=1, replica_groups=mesh['dp'=1,'tp'=4,'ep'=8] {'ep'}, dimensions={0} | all-to-all | bytes 6291456 | tf_op jit(solution)/shard_map/all_to_all | solution.py:231
  665.9 15.4 %add_convert_fusion.5 = bf16[1024,768]{1,0:T(8,128)(2,1)} fusion(bf16[4,3072,768]{2,1,0:T(8,128)(2,1)} %all-gather.26.cloned.1.call-done, f32[3072]{0:T(1024)S(1)} %bitcast.353, bf16[1024,768]{1,0:T(8,128)(2,1)} %bitcast.311, f32[768]{0:T(1024)S(1)} %get-tuple-element.55), kind=kOutput, calls=%fused_computation.98 | convolution fusion | flops 9674686464 | bytes 12598272 | tf_op jit(solution)/shard_map/dot_general | solution.py:23
  681.3 15.0 %add_convert_fusion.4 = bf16[1024,768]{1,0:T(8,128)(2,1)} fusion(bf16[4,3072,768]{2,1,0:T(8,128)(2,1)} %all-gather.26.cloned.1.call-done, f32[3072]{0:T(1024)S(1)} %bitcast.352, bf16[1024,768]{1,0:T(8,128)(2,1)S(1)} %bitcast.307, f32[768]{0:T(1024)S(1)} %get-tuple-element.58), kind=kOutput, calls=%fused_computation.97 | convolution fusion | flops 9674686464 | bytes 12598272 | tf_op jit(solution)/shard_map/dot_general | solution.py:23
  698.5 41.9 %all_to_all.22 = bf16[8,2,128,768]{3,2,1,0:T(8,128)(2,1)} all-to-all(bf16[8,2,128,768]{3,2,1,0:T(8,128)(2,1)S(1)} %pad_maximum_fusion.4), channel_id=1, replica_groups=mesh['dp'=1,'tp'=4,'ep'=8] {'ep'}, dimensions={0} | all-to-all | bytes 6291456 | tf_op jit(solution)/shard_map/all_to_all | solution.py:239
  741.4 8.5 select_reduce_fusion.1
  749.9 14.0 %fusion.123 = f32[8192,768]{0,1:T(8,128)} fusion(bf16[4096,768]{0,1:T(8,128)(2,1)} %all-gather.22.cloned.1.call-done, bf16[4096,768]{0,1:T(8,128)(2,1)} %all-gather.20.cloned.1.call-done), kind=kLoop, calls=%fused_computation.302 | loop fusion | flops 25165824 | bytes 37748736 | tf_op jit(solution)/shard_map/convert_element_type | solution.py:250
  763.9 24.7 %copy.88 = f32[8192,768]{1,0:T(8,128)} copy(f32[8192,768]{0,1:T(8,128)} %fusion.123) | data formatting | bytes 50331648 | tf_op jit(solution)/shard_map/convert_element_type | solution.py:250
  788.6 10.5 %constant_dynamic-update-slice_fusion.5 = bf16[16384,768]{1,0:T(8,128)(2,1)} fusion(bf16[8192,768]{1,0:T(8,128)(2,1)} %all-gather.24.cloned.1.call-done), kind=kLoop, calls=%fused_computation.258 | loop fusion | bytes 25165824
  799.1 59.7 %all-gather.28.cloned.1.call-done = bf16[8192,768]{1,0:T(8,128)(2,1)} async-done(((bf16[2048,768]{1,0:T(8,128)(2,1)}), bf16[8192,768]{1,0:T(8,128)(2,1)}) %all-gather.28.cloned.1.call-update) | async-done | bytes 12582928 | tf_op jit(solution)/shard_map/all_gather | solution.py:114
  858.8 10.5 %constant_dynamic-update-slice_fusion.4 = bf16[16384,768]{1,0:T(8,128)(2,1)} fusion(bf16[16384,768]{1,0:T(8,128)(2,1)} %constant_dynamic-update-slice_fusion.5, bf16[8192,768]{1,0:T(8,128)(2,1)} %all-gather.28.cloned.1.call-done), kind=kLoop, calls=%fused_computation.257 | loop fusion | bytes 25165824 | tf_op jit(solution)/shard_map/concatenate | solution.py:241
  869.3 48.4 %gather_fusion.3 = bf16[8192,768]{1,0:T(8,128)(2,1)} fusion(bf16[16384,768]{1,0:T(8,128)(2,1)} %constant_dynamic-update-slice_fusion.4, s32[8192]{0:T(1024)S(1)} %copy-done.30), kind=kCustom, calls=%fused_computation.3 | custom fusion | bytes 25198592 | tf_op jit(solution)/shard_map/gather | solution.py:248
  917.8 48.6 %gather_fusion.2 = bf16[8192,768]{1,0:T(8,128)(2,1)} fusion(bf16[16384,768]{1,0:T(8,128)(2,1)} %constant_dynamic-update-slice_fusion.4, s32[8192]{0:T(1024)S(1)} %copy-done.29), kind=kCustom, calls=%fused_computation.2 | custom fusion | bytes 25198592 | tf_op jit(solution)/shard_map/gather | solution.py:247
  966.3 22.2 %fusion.3 = bf16[8,1024,768]{2,1,0:T(8,128)(2,1)} fusion(f32[8,1024,768]{2,1,0:T(8,128)} %bitcast.283, bf16[8,1024,768]{2,1,0:T(8,128)(2,1)} %bitcast.284, bf16[8,1024,768]{2,1,0:T(8,128)(2,1)} %bitcast.285, f32[8,1024]{1,0:T(8,128)S(1)} %reshape.503, f32[8,1024]{1,0:T(8,128)S(1)} %reshape.500, pred[8,1024]{1,0:T(8,128)(4,1)S(1)} %get-tuple-element.124, ...), kind=kLoop, calls=%fused_computation.10 | loop fusion | flops 56623104 | bytes 62996480 | tf_op jit(solution)/shard_map/convert_element_type | solution.py:250
  (295 shorter events, 200.5 us)
Async XLA Ops:
  6.6 79.3 %all-gather.12.cloned.1.call-start = ((), (), s32[]{:S(2)}) async-start(), calls=%async_computation.4 | async-start | bytes 1474560 | tf_op jit(solution)/shard_map/all_gather | solution.py:129
  9.9 140.9 %all-gather.14.cloned.1.call-start = ((), (), s32[]{:S(2)}) async-start(), calls=%async_computation.5 | async-start | bytes 5898240 | tf_op jit(solution)/shard_map/all_gather | solution.py:129
  12.5 260.6 %all-gather.16.cloned.1.call-start = ((), (), s32[]{:S(2)}) async-start(), calls=%async_computation.6 | async-start | bytes 5898240 | tf_op jit(solution)/shard_map/all_gather | solution.py:129
  13.8 358.1 %all-gather.18.cloned.1.call-start = ((), (), s32[]{:S(2)}) async-start(), calls=%async_computation.7 | async-start | bytes 23592960 | tf_op jit(solution)/shard_map/all_gather | solution.py:129
  48.0 10.4 %slice-start = ((s8[6291456]{0:T(1024)(128)(4,1)}), s8[2097152]{0:T(1024)(128)(4,1)S(1)}, s32[]{:S(2)}) async-start(s8[6291456]{0:T(1024)(128)(4,1)} %bitcast.288), calls=%async_computation.13 | async-start | bytes 4194304
  63.6 21.5 %copy-start.41 = (f32[2,768]{1,0:T(2,128)S(1)}, f32[2,768]{1,0:T(2,128)}, u32[]{:S(2)}) copy-start(f32[2,768]{1,0:T(2,128)} %param.32) | copy-start | bytes 18436
  63.6 26.2 %copy-start.35 = (s32[8,1024,2]{1,2,0:T(2,128)S(1)}, s32[8,1024,2]{1,2,0:T(2,128)}, u32[]{:S(2)}) copy-start(s32[8,1024,2]{1,2,0:T(2,128)} %param.23) | copy-start | bytes 196612
  63.6 383.0 %all-gather.22.cloned.1.call-start = ((), (), s32[]{:S(2)}) async-start(), calls=%async_computation.9 | async-start | bytes 7864320 | tf_op jit(solution)/shard_map/all_gather | solution.py:114
  78.5 11.7 %copy-start.25 = (f32[4,1,4608]{2,0,1:T(4,128)}, f32[4,1,4608]{2,0,1:T(4,128)S(1)}, u32[]{:S(2)}) copy-start(f32[4,1,4608]{2,0,1:T(4,128)S(1)} %copy.116) | copy-start | bytes 221188
  85.8 62.1 %collective-permute-start.2 = (bf16[2,384,768]{2,1,0:T(8,128)(2,1)}, bf16[2,384,768]{2,1,0:T(8,128)(2,1)}, u32[]{:S(2)}, u32[]{:S(2)}) collective-permute-start(bf16[2,384,768]{2,1,0:T(8,128)(2,1)} %all-gather.12.cloned.1.call-done), channel_id=1, source_target_pairs={{0,6},{1,7},{2,0},{3,1},{4,2},{5,3},{6,4},{7,5},{8,14},{9,15},{10,... | collective-permute-start | bytes 3538952 | tf_op jit(solution)/shard_map/ppermute | solution.py:151
  88.7 56.8 %collective-permute-start.1 = (bf16[2,384,768]{2,1,0:T(8,128)(2,1)}, bf16[2,384,768]{2,1,0:T(8,128)(2,1)}, u32[]{:S(2)}, u32[]{:S(2)}) collective-permute-start(bf16[2,384,768]{2,1,0:T(8,128)(2,1)} %all-gather.12.cloned.1.call-done), channel_id=1, source_target_pairs={{0,4},{1,5},{2,6},{3,7},{4,0},{5,1},{6,2},{7,3},{8,12},{9,13},{10,... | collective-permute-start | bytes 3538952 | tf_op jit(solution)/shard_map/ppermute | solution.py:151
  89.0 54.1 %collective-permute-start = (bf16[2,384,768]{2,1,0:T(8,128)(2,1)}, bf16[2,384,768]{2,1,0:T(8,128)(2,1)}, u32[]{:S(2)}, u32[]{:S(2)}) collective-permute-start(bf16[2,384,768]{2,1,0:T(8,128)(2,1)} %all-gather.12.cloned.1.call-done), channel_id=1, source_target_pairs={{0,2},{1,3},{2,4},{3,5},{4,6},{5,7},{6,0},{7,1},{8,10},{9,11},{10,... | collective-permute-start | bytes 3538952 | tf_op jit(solution)/shard_map/ppermute | solution.py:151
  89.8 22.2 %copy-start.17 = (s32[8,1024,1]{1,2,0:T(1,128)}, s32[8,1024,1]{1,2,0:T(1,128)S(1)}, u32[]{:S(2)}) copy-start(s32[8,1024,1]{1,2,0:T(1,128)S(1)} %get-tuple-element.106) | copy-start | bytes 98308
  89.8 24.0 %copy-start.14 = (s32[8,1024,1]{1,2,0:T(1,128)}, s32[8,1024,1]{1,2,0:T(1,128)S(1)}, u32[]{:S(2)}) copy-start(s32[8,1024,1]{1,2,0:T(1,128)S(1)} %get-tuple-element.105) | copy-start | bytes 98308
  150.3 97.6 %collective-permute-start.3 = (bf16[2,1536,768]{2,1,0:T(8,128)(2,1)}, bf16[2,1536,768]{2,1,0:T(8,128)(2,1)}, u32[]{:S(2)}, u32[]{:S(2)}) collective-permute-start(bf16[2,1536,768]{2,1,0:T(8,128)(2,1)} %constant_dynamic-update-slice_fusion), channel_id=1, source_target_pairs={{0,1},{1,0},{2,3},{3,2},{4,5},{5,4},{6,7},{7,6},{8,9},{9,8},{10,11... | collective-permute-start | bytes 14155784 | tf_op jit(solution)/shard_map/ppermute | solution.py:154
  284.1 33.3 %copy-start.48 = (f32[768]{0:T(1024)S(1)}, f32[768]{0:T(1024)}, u32[]{:S(2)}) copy-start(f32[768]{0:T(1024)} %get-tuple-element.71) | copy-start | bytes 9220
  317.5 10.0 %slice-start.4 = ((s8[4718592]{0:T(1024)(128)(4,1)}), s8[524288]{0:T(1024)(128)(4,1)S(1)}, s32[]{:S(2)}) async-start(s8[4718592]{0:T(1024)(128)(4,1)} %bitcast.356), calls=%async_computation.17 | async-start | bytes 1048576
  322.5 126.7 %all-gather.20.cloned.1.call-start = ((), (), s32[]{:S(2)}) async-start(), calls=%async_computation.8 | async-start | bytes 7864320 | tf_op jit(solution)/shard_map/all_gather | solution.py:114
  371.9 8.3 copy-start.7
  371.9 8.3 copy-start.8
  371.9 8.3 copy-start.9
  380.1 285.7 %all-gather.26.cloned.1.call-start = ((), (), s32[]{:S(2)}) async-start(), calls=%async_computation.11 | async-start | bytes 23592960 | tf_op jit(solution)/shard_map/all_gather | solution.py:129
  385.5 61.0 %copy-start.31 = (pred[8192]{0:T(1024)(128)(4,1)}, pred[8192]{0:T(1024)(128)(4,1)S(1)}, u32[]{:S(2)}) copy-start(pred[8192]{0:T(1024)(128)(4,1)S(1)} %get-tuple-element.116) | copy-start | bytes 24580
  385.5 61.0 %copy-start.33 = (pred[8192]{0:T(1024)(128)(4,1)}, pred[8192]{0:T(1024)(128)(4,1)S(1)}, u32[]{:S(2)}) copy-start(pred[8192]{0:T(1024)(128)(4,1)S(1)} %get-tuple-element.76) | copy-start | bytes 24580
  449.2 8.7 copy-start.2
  449.3 8.7 copy-start.3
  502.0 42.8 %all-to-all-start = ((bf16[8,2,128,768]{3,2,1,0:T(8,128)(2,1)}), bf16[8,2,128,768]{3,2,1,0:T(8,128)(2,1)}, u32[]{:S(2)}, u32[]{:S(2)}) async-start(bf16[8,2,128,768]{3,2,1,0:T(8,128)(2,1)} %bitcast.294), calls=%async_computation | async-start | bytes 6291456 | tf_op jit(solution)/shard_map/all_to_all | solution.py:231
  507.4 281.2 %all-gather.24.cloned.1.call-start = ((), (), s32[]{:S(2)}) async-start(), calls=%async_computation.10 | async-start | bytes 15728640 | tf_op jit(solution)/shard_map/all_gather | solution.py:114
  622.4 236.4 %all-gather.28.cloned.1.call-start = ((), (), s32[]{:S(2)}) async-start(), calls=%async_computation.12 | async-start | bytes 15728640 | tf_op jit(solution)/shard_map/all_gather | solution.py:114
  799.1 70.2 %copy-start.30 = (s32[8192]{0:T(1024)S(1)}, s32[8192]{0:T(1024)}, u32[]{:S(2)}) copy-start(s32[8192]{0:T(1024)} %get-tuple-element.75) | copy-start | bytes 98308
  869.3 48.4 %copy-start.29 = (s32[8192]{0:T(1024)S(1)}, s32[8192]{0:T(1024)}, u32[]{:S(2)}) copy-start(s32[8192]{0:T(1024)} %get-tuple-element.115) | copy-start | bytes 98308
  966.3 22.3 %copy-start.1 = (bf16[768,768]{1,0:T(8,128)(2,1)S(1)}, bf16[768,768]{1,0:T(8,128)(2,1)}, u32[]{:S(2)}) copy-start(bf16[768,768]{1,0:T(8,128)(2,1)} %param.35) | copy-start | bytes 3538948
  (45 other events, 129.4 us)
Sparse Core Ops, SparseCore 0:
  10.0 23.7 all-gather.11
  35.4 52.9 all-gather.13
  90.0 50.2 all-gather.15
  141.8 170.2 all-gather.17
  322.7 61.2 all-gather.21
  385.4 63.8 all-gather.19
  450.8 170.4 all-gather.25
  622.9 116.8 all-gather.23
  741.3 117.4 all-gather.27

commit v2 on v1

--- a/solution.py
+++ b/solution.py
@@ -150,8 +150,6 @@
         for step in range(cores, ep_size, cores):
             parts.append(lax.ppermute(mine, 'ep', [(e, (e + step) % ep_size) for e in range(ep_size)]))
             owners.append((ep_me + ep_size - step) % ep_size)
-        core_half = jnp.concatenate(parts, axis=1)
-        other_half = lax.ppermute(core_half, 'ep', [(e, e ^ 1) for e in range(ep_size)])
         owners = jnp.stack(owners)
         b_slabs = b_in.reshape(tp_size, ep_size, slab).transpose(1, 0, 2)
 
@@ -172,7 +170,6 @@
             return [(both[2 * i], both[2 * i + 1]) for i in range(len(experts))], after
 
 
-        dense_blocks = [(core_half[0], slab_bias(owners), core_half[1]), (other_half[0], slab_bias(other_owners), other_half[1])]
         first_weights = qkvo[0], qkvo[1], qkvo[2], qkvo[3]
 
         own_x = lax.dynamic_index_in_dim(x.reshape(own_rows, tp_size, seq_len, d_model), me, 1, keepdims=False).reshape(own_rows * seq_len, d_model)
@@ -196,6 +193,10 @@
         table = jnp.zeros((dump_slot + 1,), jnp.int32)
         own_normed, slot_first, slot_second = lax.optimization_barrier((own_normed, slot_first, slot_second))
         own = attention(own_x, own_normed, own_len, 0, first_weights)
+        parts, own = lax.optimization_barrier((parts, own))
+        core_half = jnp.concatenate(parts, axis=1)
+        other_half = lax.ppermute(core_half, 'ep', [(e, e ^ 1) for e in range(ep_size)])
+        dense_blocks = [(core_half[0], slab_bias(owners), core_half[1]), (other_half[0], slab_bias(other_owners), other_half[1])]
         own = dense_ffn(own, ln_gain[1], ln_bias[1], dense_blocks, b_fc2)
         chunks = []
         for c in range(own_rows):

time: 1000 us -> 996 us (level)
  local copies, waits for them, and re-layouts: 320 us -> 264 us
  waiting for transfers between devices: 110 us -> 135 us
  other arithmetic: 114 us -> 135 us
    all_gather x4, waiting for transfers between devices: 62.4 us -> 114 us  [gathered(): return lax.all_gather(shard, 'tp', axis=0, tiled=True)]
    convert_element_type x2 -> x0, local copies, waits for them, and re-layouts: 41.3 us -> none  [the longest x1 24.7 us: local_fn(): hidden.astype(jnp.float32) + combined]
    ppermute x3, waiting for transfers between devices: 26.7 us -> 0.01 us  [local_fn(): lax.ppermute(mine, 'ep', [(e, (e + step) % ep_size) for e in range(ep_siz...]
    unnamed x142 -> x129, local copies, waits for them, and re-layouts: 42.5 us -> 31 us
  transfers between devices with their start and end apart: 14 -> 14, of which waited for: 4 -> 3; matrix products, arithmetic and copies ran while one was open for 46% -> 43% of each run, Pallas kernels for 13% -> 13%
where the time goes in v2:
time: 996 us; the launch traced here: 988 us
  local copies, waits for them, and re-layouts  264 us (27%)
  matrix products  157 us (16%)
  blocking collectives  138 us (14%)
  other arithmetic  135 us (14%)
  waiting for transfers between devices  135 us (14%)
  Pallas kernels  131 us (13%)
  starting transfers between devices  14.4 us (1%)
  between operations  14.4 us (1%)
    pallas_call x3, Pallas kernels, attend(): pl.pallas_call(functools.partial(attention_kernel, head_dim, 256), out_sh...  131 us
    all_gather x4, waiting for transfers between devices, gathered(): return lax.all_gather(shard, 'tp', axis=0, tiled=True)  114 us
    dot_general x9, matrix products, dot_rows(): lax.dot_general(lhs, rhs, (((1,), (0,)), ((), ())), preferred_element_typ...  91.9 us
    all_to_all x2, blocking collectives, local_fn(): back = lax.all_to_all(jnp.stack(outs, axis=1), 'ep', 0, 0, tiled=True)  83.6 us
    dot_general x11, matrix products, dot_cols(): lax.dot_general(lhs, rhs, (((1,), (1,)), ((), ())), preferred_element_typ...  52.7 us
    gather x1, local copies, waits for them, and re-layouts, local_fn(): flat[jnp.where(keep_second, place(second, slot_second), 0)]  48.4 us
    gather x1, local copies, waits for them, and re-layouts, local_fn(): flat[jnp.where(keep_first, place(first, slot_first), 0)].astype(jnp.float32)  48.4 us
    all_to_all x1, blocking collectives, local_fn(): received = lax.all_to_all(dispatch[n], 'ep', 0, 0, tiled=True)  42 us
  transfers between devices with their start and end apart: 14, of which 3 were waited for; matrix products, arithmetic and copies ran while one was open for 43% of the time, Pallas kernels for 13%

profile of v2, /device:TPU:97, one launch (start us, length us, event | category | flops | bytes accessed | tf_op | source)
XLA Modules:
  0.0 988.0 jit_solution(17105965356993013698)
XLA Ops:
  40.1 12.6 %all-gather.1 = f32[4,1,4608]{2,1,0:T(1,128)S(1)} all-gather(f32[1,1,4608]{2,1,0:T(1,128)S(1)} %reshape.558), channel_id=2, replica_groups=mesh['dp'=1,'tp'=4,'ep'=8] {'tp'}, dimensions={0}, use_global_device_ids=true | all-gather | bytes 92160 | tf_op jit(solution)/shard_map/all_gather | solution.py:135
  64.1 9.5 reduce-window.16
  74.8 17.1 %reduce-window.14 = s32[32,64,128]{2,1,0:T(8,128)S(1)} reduce-window(s32[32,64,128]{2,1,0:T(8,128)} %get-tuple-element.128, s32[]{:T(128)} %constant.212.clone.1), window={size=1x1x128 pad=0_0x0_0x127_0}, to_apply=%region_2.3 | reduce-window | flops 33292288 | bytes 2097156 | tf_op jit(solution)/shard_map/reduce-window
  111.4 64.1 %attend.3 = bf16[2048,768]{1,0:T(8,128)(2,1)} custom-call(s32[2]{0:T(128)} %get-tuple-element.87.len_ref, bf16[2048,768]{1,0:T(8,128)(2,1)} %add_convert_fusion.1.q_ref, bf16[2048,768]{1,0:T(8,128)(2,1)} %convolution_convert_fusion.k_ref, bf16[2048,768]{1,0:T(8,128)(2,1)} %add_convert_fusion.v_ref), custom_call_target="tpu_custom_call" | custom-call | flops 64424509440 | bytes 12582912 | tf_op jit(solution)/shard_map/attend/pallas_call | solution.py:71
  175.5 7.6 fusion.31
  246.2 33.2 %attend.5 = bf16[1024,768]{1,0:T(8,128)(2,1)} custom-call(s32[1]{0:T(128)} %bitcast.73.len_ref, bf16[1024,768]{1,0:T(8,128)(2,1)} %add_convert_fusion.7.q_ref, bf16[1024,768]{1,0:T(8,128)(2,1)} %convolution_convert_fusion.1.k_ref, bf16[1024,768]{1,0:T(8,128)(2,1)} %add_convert_fusion.6.v_ref), custom_call_target="tpu_custom_call" | custom-call | flops 32212254720 | bytes 6291456 | tf_op jit(solution)/shard_map/attend/pallas_call | solution.py:71
  297.4 33.2 %attend.4 = bf16[1024,768]{1,0:T(8,128)(2,1)} custom-call(s32[1]{0:T(128)} %bitcast.46.len_ref, bf16[1024,768]{1,0:T(8,128)(2,1)} %add_convert_fusion.9.q_ref, bf16[1024,768]{1,0:T(8,128)(2,1)} %convolution_convert_fusion.2.k_ref, bf16[1024,768]{1,0:T(8,128)(2,1)} %add_convert_fusion.8.v_ref), custom_call_target="tpu_custom_call" | custom-call | flops 32212254720 | bytes 6291456 | tf_op jit(solution)/shard_map/attend/pallas_call | solution.py:71
  335.4 8.1 slice_bitcast_fusion.12
  349.3 30.5 %scatter_custom_fusion = s32[16385]{0:T(1024)S(1)} fusion(s32[8192]{0:T(1024)S(1)} %get-tuple-element.124, s32[8192]{0:T(1024)S(1)} %iota.35, s32[]{:T(128)} %constant.212.clone.1), kind=kCustom, calls=%fused_computation.201 | custom fusion | bytes 65544 | tf_op jit(solution)/shard_map/scatter | solution.py:212
  379.8 30.5 %scatter_fusion = s32[16385]{0:T(1024)S(1)} fusion(s32[16385]{0:T(1024)S(1)} %scatter_custom_fusion, s32[8192]{0:T(1024)S(1)} %get-tuple-element.123, s32[8192]{0:T(1024)S(1)} %iota.36), kind=kCustom, calls=%fused_computation.5 | custom fusion | bytes 131072 | tf_op jit(solution)/shard_map/scatter | solution.py:213
  410.4 31.6 %all-gather.20.cloned.1.call-done = bf16[4096,768]{1,0:T(8,128)(2,1)} async-done(((bf16[1024,768]{1,0:T(8,128)(2,1)}), bf16[4096,768]{1,0:T(8,128)(2,1)}) %all-gather.20.cloned.1.call-update) | async-done | bytes 6291472 | tf_op jit(solution)/shard_map/all_gather | solution.py:114
  442.0 8.9 convert_reduce_fusion
  451.0 11.7 %multiply_reduce_fusion = f32[8192]{0:T(1024)S(1)} fusion(f32[8192]{0:T(1024)S(1)} %broadcast_multiply_fusion, bf16[4096,768]{1,0:T(8,128)(2,1)S(1)} %copy-done.2, bf16[4096,768]{1,0:T(8,128)(2,1)S(1)} %copy-done.3), kind=kLoop, calls=%fused_computation.14 | loop fusion | flops 44032000 | bytes 12648448 | tf_op jit(solution)/shard_map/reduce_sum | solution.py:18
  462.8 13.8 %fusion.5 = bf16[8192,768]{1,0:T(8,128)(2,1)} fusion(f32[768]{0:T(1024)S(1)} %copy-done.38, f32[768]{0:T(1024)S(1)} %copy-done.39, f32[8192]{0:T(1024)S(1)} %add_rsqrt_fusion, f32[8192]{0:T(1024)S(1)} %broadcast_multiply_fusion, bf16[4096,768]{1,0:T(8,128)(2,1)S(1)} %copy-done.2, bf16[4096,768]{1,0:T(8,128)(2,1)S(1)} %copy-done.3), kind=kLoop, calls=%fused_computation.15 | loop fusion | flops 56623104 | bytes 25237504 | tf_op jit(solution)/shard_map/convert_element_type | solution.py:226
  476.6 16.3 %gather_fusion = bf16[2048,768]{1,0:T(8,128)(2,1)} fusion(bf16[8192,768]{1,0:T(8,128)(2,1)} %fusion.5, s32[2048]{0:T(1024)S(1)} %broadcast_clamp_fusion.1), kind=kCustom, calls=%fused_computation | custom fusion | bytes 6299648 | tf_op jit(solution)/shard_map/gather | solution.py:230
  498.4 16.4 %gather_fusion.1 = bf16[2048,768]{1,0:T(8,128)(2,1)} fusion(bf16[8192,768]{1,0:T(8,128)(2,1)} %fusion.5, s32[2048]{0:T(1024)S(1)} %broadcast_clamp_fusion), kind=kCustom, calls=%fused_computation.1 | custom fusion | bytes 6299648 | tf_op jit(solution)/shard_map/gather | solution.py:230
  514.8 20.8 %all-to-all-done = bf16[8,2,128,768]{3,2,1,0:T(8,128)(2,1)} async-done(((bf16[8,2,128,768]{3,2,1,0:T(8,128)(2,1)}), bf16[8,2,128,768]{3,2,1,0:T(8,128)(2,1)}, u32[]{:S(2)}, u32[]{:S(2)}) %all-to-all-start) | async-done | bytes 3145760 | tf_op jit(solution)/shard_map/all_to_all | solution.py:232
  538.9 15.5 %add_convert_fusion.5 = bf16[1024,768]{1,0:T(8,128)(2,1)} fusion(bf16[3072,768]{1,0:T(8,128)(2,1)} %get-tuple-element.49, f32[3072]{0:T(1024)S(1)} %bitcast.364, bf16[1024,768]{1,0:T(8,128)(2,1)} %bitcast.322, bf16[3072,768]{1,0:T(8,128)(2,1)} %get-tuple-element.48, f32[768]{0:T(1024)S(1)} %get-tuple-element.67), kind=kOutput, calls=%fused_computation.108 | convolution fusion | flops 9674686464 | bytes 12598272 | tf_op jit(solution)/shard_map/dot_general | solution.py:23
  554.4 15.0 %add_convert_fusion.4 = bf16[1024,768]{1,0:T(8,128)(2,1)} fusion(bf16[4,3072,768]{2,1,0:T(8,128)(2,1)} %all-gather.18.cloned.1.call-done, f32[3072]{0:T(1024)S(1)} %bitcast.363, bf16[1024,768]{1,0:T(8,128)(2,1)S(1)} %bitcast.318, f32[768]{0:T(1024)S(1)} %get-tuple-element.66), kind=kOutput, calls=%fused_computation.107 | convolution fusion | flops 9674686464 | bytes 12598272 | tf_op jit(solution)/shard_map/dot_general | solution.py:23
  571.6 41.7 %all_to_all.20 = bf16[8,2,128,768]{3,2,1,0:T(8,128)(2,1)} all-to-all(bf16[8,2,128,768]{3,2,1,0:T(8,128)(2,1)S(1)} %pad_maximum_fusion.3), channel_id=1, replica_groups=mesh['dp'=1,'tp'=4,'ep'=8] {'ep'}, dimensions={0} | all-to-all | bytes 6291456 | tf_op jit(solution)/shard_map/all_to_all | solution.py:240
  613.4 42.0 %all_to_all.21 = bf16[8,2,128,768]{3,2,1,0:T(8,128)(2,1)S(1)} all-to-all(bf16[8,2,128,768]{3,2,1,0:T(8,128)(2,1)} %bitcast.305), channel_id=1, replica_groups=mesh['dp'=1,'tp'=4,'ep'=8] {'ep'}, dimensions={0} | all-to-all | bytes 6291456 | tf_op jit(solution)/shard_map/all_to_all | solution.py:232
  656.8 15.5 %add_convert_fusion.3 = bf16[1024,768]{1,0:T(8,128)(2,1)} fusion(bf16[4,3072,768]{2,1,0:T(8,128)(2,1)} %all-gather.26.cloned.1.call-done, f32[3072]{0:T(1024)S(1)} %bitcast.362, bf16[1024,768]{1,0:T(8,128)(2,1)} %bitcast.321, f32[768]{0:T(1024)S(1)} %get-tuple-element.65), kind=kOutput, calls=%fused_computation.106 | convolution fusion | flops 9674686464 | bytes 12598272 | tf_op jit(solution)/shard_map/dot_general | solution.py:23
  672.2 15.0 %add_convert_fusion.2 = bf16[1024,768]{1,0:T(8,128)(2,1)} fusion(bf16[4,3072,768]{2,1,0:T(8,128)(2,1)} %all-gather.26.cloned.1.call-done, f32[3072]{0:T(1024)S(1)} %bitcast.361, bf16[1024,768]{1,0:T(8,128)(2,1)S(1)} %bitcast.317, f32[768]{0:T(1024)S(1)} %get-tuple-element.68), kind=kOutput, calls=%fused_computation.105 | convolution fusion | flops 9674686464 | bytes 12598272 | tf_op jit(solution)/shard_map/dot_general | solution.py:23
  689.4 42.0 %all_to_all.22 = bf16[8,2,128,768]{3,2,1,0:T(8,128)(2,1)} all-to-all(bf16[8,2,128,768]{3,2,1,0:T(8,128)(2,1)S(1)} %pad_maximum_fusion.4), channel_id=1, replica_groups=mesh['dp'=1,'tp'=4,'ep'=8] {'ep'}, dimensions={0} | all-to-all | bytes 6291456 | tf_op jit(solution)/shard_map/all_to_all | solution.py:240
  732.3 12.0 %select_reduce_fusion.1 = (f32[8192]{0:T(1024)S(1)}, f32[8192]{0:T(1024)S(1)}) fusion(s32[8192]{0:T(1024)S(1)} %bitcast.342, s32[8192]{0:T(1024)S(1)} %bitcast.337, f32[768,32]{0,1:T(8,128)S(1)} %copy-done.55, f32[768]{0:T(1024)S(1)} %copy-done.38, f32[768]{0:T(1024)S(1)} %copy-done.39, f32[8192]{0:T(1024)S(1)} %add_rsqrt_fusion, ...), kind=kOutput, calls=%fused_computation.146 | convolution fusion | flops 454541312 | bytes 12883968 | tf_op jit(solution)/shard_map/dot_general | solution.py:219
  744.4 14.4 %fusion.131 = f32[8192,768]{1,0:T(8,128)} fusion(bf16[4096,768]{1,0:T(8,128)(2,1)} %all-gather.22.cloned.1.call-done, bf16[4096,768]{1,0:T(8,128)(2,1)} %all-gather.20.cloned.1.call-done), kind=kLoop, calls=%fused_computation.310 | loop fusion | flops 25165824 | bytes 37748736 | tf_op jit(solution)/shard_map/convert_element_type | solution.py:251
  758.9 10.6 %constant_dynamic-update-slice_fusion.5 = bf16[16384,768]{1,0:T(8,128)(2,1)} fusion(bf16[8192,768]{1,0:T(8,128)(2,1)} %all-gather.24.cloned.1.call-done), kind=kLoop, calls=%fused_computation.267 | loop fusion | bytes 25165824
  769.5 82.1 %all-gather.28.cloned.1.call-done = bf16[8192,768]{1,0:T(8,128)(2,1)} async-done(((bf16[2048,768]{1,0:T(8,128)(2,1)}), bf16[8192,768]{1,0:T(8,128)(2,1)}) %all-gather.28.cloned.1.call-update) | async-done | bytes 12582928 | tf_op jit(solution)/shard_map/all_gather | solution.py:114
  851.6 10.6 %constant_dynamic-update-slice_fusion.4 = bf16[16384,768]{1,0:T(8,128)(2,1)} fusion(bf16[16384,768]{1,0:T(8,128)(2,1)} %constant_dynamic-update-slice_fusion.5, bf16[8192,768]{1,0:T(8,128)(2,1)} %all-gather.28.cloned.1.call-done), kind=kLoop, calls=%fused_computation.266 | loop fusion | bytes 25165824 | tf_op jit(solution)/shard_map/concatenate | solution.py:242
  862.1 48.4 %gather_fusion.3 = bf16[8192,768]{1,0:T(8,128)(2,1)} fusion(bf16[16384,768]{1,0:T(8,128)(2,1)} %constant_dynamic-update-slice_fusion.4, s32[8192]{0:T(1024)S(1)} %copy-done.32), kind=kCustom, calls=%fused_computation.3 | custom fusion | bytes 25198592 | tf_op jit(solution)/shard_map/gather | solution.py:249
  910.6 48.4 %gather_fusion.2 = bf16[8192,768]{1,0:T(8,128)(2,1)} fusion(bf16[16384,768]{1,0:T(8,128)(2,1)} %constant_dynamic-update-slice_fusion.4, s32[8192]{0:T(1024)S(1)} %copy-done.31), kind=kCustom, calls=%fused_computation.2 | custom fusion | bytes 25198592 | tf_op jit(solution)/shard_map/gather | solution.py:248
  959.0 22.2 %fusion.3 = bf16[8,1024,768]{2,1,0:T(8,128)(2,1)} fusion(f32[8,1024,768]{2,1,0:T(8,128)} %bitcast.296, bf16[8,1024,768]{2,1,0:T(8,128)(2,1)} %bitcast.297, bf16[8,1024,768]{2,1,0:T(8,128)(2,1)} %bitcast.298, f32[8,1024]{1,0:T(8,128)S(1)} %reshape.503, f32[8,1024]{1,0:T(8,128)S(1)} %reshape.500, pred[8,1024]{1,0:T(8,128)(4,1)S(1)} %get-tuple-element.134, ...), kind=kLoop, calls=%fused_computation.10 | loop fusion | flops 56623104 | bytes 62996480 | tf_op jit(solution)/shard_map/convert_element_type | solution.py:251
  (276 shorter events, 172.4 us)
Async XLA Ops:
  6.6 51.8 %all-gather.12.cloned.1.call-start = ((), (), s32[]{:S(2)}) async-start(), calls=%async_computation.4 | async-start | bytes 1474560 | tf_op jit(solution)/shard_map/all_gather | solution.py:129
  9.9 86.8 %all-gather.14.cloned.1.call-start = ((), (), s32[]{:S(2)}) async-start(), calls=%async_computation.5 | async-start | bytes 5898240 | tf_op jit(solution)/shard_map/all_gather | solution.py:129
  12.5 223.2 %all-gather.16.cloned.1.call-start = ((), (), s32[]{:S(2)}) async-start(), calls=%async_computation.6 | async-start | bytes 5898240 | tf_op jit(solution)/shard_map/all_gather | solution.py:129
  13.8 321.6 %all-gather.18.cloned.1.call-start = ((), (), s32[]{:S(2)}) async-start(), calls=%async_computation.7 | async-start | bytes 23592960 | tf_op jit(solution)/shard_map/all_gather | solution.py:129
  38.4 15.5 %copy-start.44 = (f32[2,768]{1,0:T(2,128)S(1)}, f32[2,768]{1,0:T(2,128)}, u32[]{:S(2)}) copy-start(f32[2,768]{1,0:T(2,128)} %param.32) | copy-start | bytes 18436
  38.4 372.0 %all-gather.22.cloned.1.call-start = ((), (), s32[]{:S(2)}) async-start(), calls=%async_computation.9 | async-start | bytes 7864320 | tf_op jit(solution)/shard_map/all_gather | solution.py:114
  52.7 142.2 %copy-start.27 = (f32[4,1,4608]{2,0,1:T(4,128)}, f32[4,1,4608]{2,0,1:T(4,128)S(1)}, u32[]{:S(2)}) copy-start(f32[4,1,4608]{2,0,1:T(4,128)S(1)} %copy.102) | copy-start | bytes 221188
  58.4 124.8 %collective-permute-start.2 = (bf16[2,384,768]{2,1,0:T(8,128)(2,1)}, bf16[2,384,768]{2,1,0:T(8,128)(2,1)}, u32[]{:S(2)}, u32[]{:S(2)}) collective-permute-start(bf16[2,384,768]{2,1,0:T(8,128)(2,1)} %all-gather.12.cloned.1.call-done), channel_id=1, source_target_pairs={{0,6},{1,7},{2,0},{3,1},{4,2},{5,3},{6,4},{7,5},{8,14},{9,15},{10,... | collective-permute-start | bytes 3538952 | tf_op jit(solution)/shard_map/ppermute | solution.py:151
  61.2 121.9 %collective-permute-start.1 = (bf16[2,384,768]{2,1,0:T(8,128)(2,1)}, bf16[2,384,768]{2,1,0:T(8,128)(2,1)}, u32[]{:S(2)}, u32[]{:S(2)}) collective-permute-start(bf16[2,384,768]{2,1,0:T(8,128)(2,1)} %all-gather.12.cloned.1.call-done), channel_id=1, source_target_pairs={{0,4},{1,5},{2,6},{3,7},{4,0},{5,1},{6,2},{7,3},{8,12},{9,13},{10,... | collective-permute-start | bytes 3538952 | tf_op jit(solution)/shard_map/ppermute | solution.py:151
  61.6 121.5 %collective-permute-start = (bf16[2,384,768]{2,1,0:T(8,128)(2,1)}, bf16[2,384,768]{2,1,0:T(8,128)(2,1)}, u32[]{:S(2)}, u32[]{:S(2)}) collective-permute-start(bf16[2,384,768]{2,1,0:T(8,128)(2,1)} %all-gather.12.cloned.1.call-done), channel_id=1, source_target_pairs={{0,2},{1,3},{2,4},{3,5},{4,6},{5,7},{6,0},{7,1},{8,10},{9,11},{10,... | collective-permute-start | bytes 3538952 | tf_op jit(solution)/shard_map/ppermute | solution.py:151
  62.8 30.6 %copy-start.19 = (s32[8,1024,1]{1,2,0:T(1,128)}, s32[8,1024,1]{1,2,0:T(1,128)S(1)}, u32[]{:S(2)}) copy-start(s32[8,1024,1]{1,2,0:T(1,128)S(1)} %get-tuple-element.116) | copy-start | bytes 98308
  62.9 32.4 %copy-start.16 = (s32[8,1024,1]{1,2,0:T(1,128)}, s32[8,1024,1]{1,2,0:T(1,128)S(1)}, u32[]{:S(2)}) copy-start(s32[8,1024,1]{1,2,0:T(1,128)S(1)} %get-tuple-element.115) | copy-start | bytes 98308
  184.2 11.5 %copy-start.10 = (bf16[1,768,768]{2,1,0:T(8,128)(2,1)S(1)}, bf16[1,768,768]{2,1,0:T(8,128)(2,1)}, u32[]{:S(2)}) copy-start(bf16[1,768,768]{2,1,0:T(8,128)(2,1)} %get-tuple-element.96) | copy-start | bytes 3538948
  191.4 27.6 %collective-permute-start.3 = (bf16[2,1536,768]{2,1,0:T(8,128)(2,1)}, bf16[2,1536,768]{2,1,0:T(8,128)(2,1)}, u32[]{:S(2)}, u32[]{:S(2)}) collective-permute-start(bf16[2,1536,768]{2,1,0:T(8,128)(2,1)} %constant_dynamic-update-slice_fusion), channel_id=1, source_target_pairs={{0,1},{1,0},{2,3},{3,2},{4,5},{5,4},{6,7},{7,6},{8,9},{9,8},{10,11... | collective-permute-start | bytes 14155784 | tf_op jit(solution)/shard_map/ppermute | solution.py:198
  246.2 33.2 %copy-start.50 = (f32[768]{0:T(1024)S(1)}, f32[768]{0:T(1024)}, u32[]{:S(2)}) copy-start(f32[768]{0:T(1024)} %get-tuple-element.81) | copy-start | bytes 9220
  284.3 157.8 %all-gather.20.cloned.1.call-start = ((), (), s32[]{:S(2)}) async-start(), calls=%async_computation.8 | async-start | bytes 7864320 | tf_op jit(solution)/shard_map/all_gather | solution.py:114
  335.4 8.7 copy-start.8
  335.4 8.7 copy-start.9
  335.4 8.7 copy-start.11
  343.6 313.2 %all-gather.26.cloned.1.call-start = ((), (), s32[]{:S(2)}) async-start(), calls=%async_computation.11 | async-start | bytes 23592960 | tf_op jit(solution)/shard_map/all_gather | solution.py:129
  349.3 61.0 %copy-start.33 = (pred[8192]{0:T(1024)(128)(4,1)}, pred[8192]{0:T(1024)(128)(4,1)S(1)}, u32[]{:S(2)}) copy-start(pred[8192]{0:T(1024)(128)(4,1)S(1)} %get-tuple-element.126) | copy-start | bytes 24580
  349.3 61.0 %copy-start.35 = (pred[8192]{0:T(1024)(128)(4,1)}, pred[8192]{0:T(1024)(128)(4,1)S(1)}, u32[]{:S(2)}) copy-start(pred[8192]{0:T(1024)(128)(4,1)S(1)} %get-tuple-element.86) | copy-start | bytes 24580
  442.0 8.9 copy-start.2
  442.0 8.9 copy-start.3
  451.0 11.8 %copy-start.38 = (f32[768]{0:T(1024)S(1)}, f32[768]{0:T(1024)}, u32[]{:S(2)}) copy-start(f32[768]{0:T(1024)} %get-tuple-element.73) | copy-start | bytes 9220
  451.0 11.8 %copy-start.39 = (f32[768]{0:T(1024)S(1)}, f32[768]{0:T(1024)}, u32[]{:S(2)}) copy-start(f32[768]{0:T(1024)} %get-tuple-element.142) | copy-start | bytes 9220
  492.8 42.8 %all-to-all-start = ((bf16[8,2,128,768]{3,2,1,0:T(8,128)(2,1)}), bf16[8,2,128,768]{3,2,1,0:T(8,128)(2,1)}, u32[]{:S(2)}, u32[]{:S(2)}) async-start(bf16[8,2,128,768]{3,2,1,0:T(8,128)(2,1)} %bitcast.306), calls=%async_computation | async-start | bytes 6291456 | tf_op jit(solution)/shard_map/all_to_all | solution.py:232
  498.2 260.7 %all-gather.24.cloned.1.call-start = ((), (), s32[]{:S(2)}) async-start(), calls=%async_computation.10 | async-start | bytes 15728640 | tf_op jit(solution)/shard_map/all_gather | solution.py:114
  613.3 238.3 %all-gather.28.cloned.1.call-start = ((), (), s32[]{:S(2)}) async-start(), calls=%async_computation.12 | async-start | bytes 15728640 | tf_op jit(solution)/shard_map/all_gather | solution.py:114
  769.5 92.7 %copy-start.32 = (s32[8192]{0:T(1024)S(1)}, s32[8192]{0:T(1024)}, u32[]{:S(2)}) copy-start(s32[8192]{0:T(1024)} %get-tuple-element.85) | copy-start | bytes 98308
  862.1 48.4 %copy-start.31 = (s32[8192]{0:T(1024)S(1)}, s32[8192]{0:T(1024)}, u32[]{:S(2)}) copy-start(s32[8192]{0:T(1024)} %get-tuple-element.125) | copy-start | bytes 98308
  959.0 22.3 %copy-start.1 = (bf16[768,768]{1,0:T(8,128)(2,1)S(1)}, bf16[768,768]{1,0:T(8,128)(2,1)}, u32[]{:S(2)}) copy-start(bf16[768,768]{1,0:T(8,128)(2,1)} %param.35) | copy-start | bytes 3538948
  (39 other events, 118.9 us)
Sparse Core Ops, SparseCore 0:
  10.0 23.6 all-gather.11
  35.3 52.8 all-gather.13
  89.8 50.2 all-gather.15
  141.6 170.2 all-gather.17
  313.3 63.4 all-gather.21
  378.2 63.7 all-gather.19
  443.6 170.4 all-gather.25
  615.6 116.8 all-gather.23
  734.0 117.4 all-gather.27
